TPU v7x, 8 devices: a whole 2x2x1 slice. The times are simulated.
8 devices in a mesh: dp: 2 (over z, y), tp: 4 (over x, core).
Axes of the slice: x: 2, y: 2, z: 1, core: 2. Of those that a mesh axis runs over, the one named last changes fastest.
Arguments:
- hidden_in: bfloat16 [2048, 2048], P(('dp', 'tp')), parts along dimension 0
- k_cache: bfloat16 [2048, 512, 256], P(('dp', 'tp')), parts along dimension 0
- v_cache: bfloat16 [2048, 512, 256], P(('dp', 'tp')), parts along dimension 0
- cache_len: int32 [2048], P(('dp', 'tp')), parts along dimension 0
- norm_attn: bfloat16 [2048], replicated
- norm_mlp: bfloat16 [2048], replicated
- w_q: bfloat16 [2048, 2048], replicated
- w_k: bfloat16 [2048, 256], replicated
- w_v: bfloat16 [2048, 256], replicated
- w_o: bfloat16 [2048, 2048], replicated
- w_gate: bfloat16 [2048, 16384], P(None, 'tp')
- w_up: bfloat16 [2048, 16384], P(None, 'tp')
- w_down: bfloat16 [16384, 2048], P('tp')
Outputs:
- output 1: bfloat16 [2048, 2048], P(('dp', 'tp')), parts along dimension 0
- output 2: bfloat16 [2048, 256], P(('dp', 'tp')), parts along dimension 0
- output 3: bfloat16 [2048, 256], P(('dp', 'tp')), parts along dimension 0
There are 2 independent parts. A program takes and returns all parts, laid end to end along the dimension named above; an argument that names none is the same for every part.
All inputs are finite; a program needn't handle non-finite values.
Results may differ from a plain program's by a relative error of at most 0.00565983.
Values are sent between devices in bfloat16 or wider.
A program may use at most 1 GiB of HBM per device.

v0:
```python
import jax
import jax.numpy as jnp
from jax import lax
from jax.sharding import PartitionSpec as P


def rms_scale(values, gain_vec):
    wide_vals = values.astype(jnp.float32)
    inv_rms = lax.rsqrt(jnp.mean(wide_vals * wide_vals, axis=-1, keepdims=True) + 1e-6)
    return (wide_vals * inv_rms * (1.0 + gain_vec.astype(jnp.float32))).astype(jnp.bfloat16)


def rope_tables(positions, head_dim):
    half_dim = head_dim // 2
    inv_freq = 10000.0 ** (-2.0 * jnp.arange(half_dim, dtype=jnp.float32) / head_dim)
    angles = positions.astype(jnp.float32)[:, None] * inv_freq[None, :]
    return jnp.cos(angles), jnp.sin(angles)


def rotary(values, cos_t, sin_t):
    half_dim = values.shape[-1] // 2
    first_half = values[..., :half_dim]
    second_half = values[..., half_dim:]
    return jnp.concatenate([first_half * cos_t - second_half * sin_t, second_half * cos_t + first_half * sin_t], axis=-1)


def attend(q_rot, k_new, v_new, k_cache, v_cache, cache_len):
    hist_score = jnp.einsum('bhd,btd->bht', q_rot, k_cache, preferred_element_type=jnp.float32)
    new_score = jnp.einsum('bhd,bd->bh', q_rot, k_new, preferred_element_type=jnp.float32)
    valid_mask = lax.broadcasted_iota(jnp.int32, (1, 1, k_cache.shape[1]), 2) < cache_len[:, None, None]
    hist_score = jnp.where(valid_mask, hist_score, -jnp.inf)
    peak_score = jnp.maximum(jnp.max(hist_score, axis=-1), new_score)
    hist_weight = jnp.exp(hist_score - peak_score[..., None])
    new_weight = jnp.exp(new_score - peak_score)
    weight_sum = jnp.sum(hist_weight, axis=-1) + new_weight
    hist_prob = (hist_weight / weight_sum[..., None]).astype(jnp.bfloat16)
    new_prob = (new_weight / weight_sum).astype(jnp.bfloat16)
    attn_out = jnp.einsum('bht,btd->bhd', hist_prob, v_cache, preferred_element_type=jnp.float32)
    attn_out = attn_out + new_prob.astype(jnp.float32)[..., None] * v_new.astype(jnp.float32)[:, None, :]
    return attn_out.astype(jnp.bfloat16)


def attention_block(hidden_in, k_cache, v_cache, cache_len, norm_attn, w_q, w_k, w_v, w_o):
    num_rows = hidden_in.shape[0]
    head_dim = w_k.shape[1]
    num_heads = w_q.shape[1] // head_dim
    normed = rms_scale(hidden_in, norm_attn)
    q_lin = jnp.dot(normed, w_q, preferred_element_type=jnp.float32).reshape(num_rows, num_heads, head_dim)
    k_lin = jnp.dot(normed, w_k, preferred_element_type=jnp.float32)
    v_new = jnp.dot(normed, w_v, preferred_element_type=jnp.float32).astype(jnp.bfloat16)
    cos_t, sin_t = rope_tables(cache_len, head_dim)
    q_rot = (rotary(q_lin, cos_t[:, None, :], sin_t[:, None, :]) * head_dim ** -0.5).astype(jnp.bfloat16)
    k_new = rotary(k_lin, cos_t, sin_t).astype(jnp.bfloat16)
    attn_out = attend(q_rot, k_new, v_new, k_cache, v_cache, cache_len)
    mixed = jnp.dot(attn_out.reshape(num_rows, num_heads * head_dim), w_o, preferred_element_type=jnp.float32)
    return hidden_in.astype(jnp.float32) + mixed, k_new, v_new


def solution(mesh):
    row_spec = P(('dp', 'tp'), None)
    cache_spec = P(('dp', 'tp'), None, None)
    full_vec = P(None)
    full_mat = P(None, None)

    def per_device(hidden_in, k_cache, v_cache, cache_len, norm_attn, norm_mlp, w_q, w_k, w_v, w_o, w_gate, w_up, w_down):
        x_mid, k_new, v_new = attention_block(hidden_in, k_cache, v_cache, cache_len, norm_attn, w_q, w_k, w_v, w_o)
        xn_mid = rms_scale(x_mid, norm_mlp)
        group_rows = lax.all_gather(xn_mid, 'tp', axis=0, tiled=True)
        gate_act = jnp.dot(group_rows, w_gate, preferred_element_type=jnp.float32)
        up_act = jnp.dot(group_rows, w_up, preferred_element_type=jnp.float32)
        hidden_act = (jax.nn.gelu(gate_act, approximate=True) * up_act).astype(jnp.bfloat16)
        part_sum = jnp.dot(hidden_act, w_down, preferred_element_type=jnp.float32)
        down_sum = lax.psum_scatter(part_sum, 'tp', scatter_dimension=0, tiled=True)
        return (x_mid + down_sum).astype(jnp.bfloat16), k_new, v_new

    return jax.shard_map(
        per_device,
        mesh=mesh,
        in_specs=(row_spec, cache_spec, cache_spec, P(('dp', 'tp')), full_vec, full_vec,
                  full_mat, full_mat, full_mat, full_mat, P(None, 'tp'), P(None, 'tp'), P('tp', None)),
        out_specs=(row_spec, row_spec, row_spec),
        check_vma=False,
    )
```

profile of v0, /device:TPU:0, one launch (start us, length us, event | category | flops | bytes accessed | tf_op | source)
XLA Modules:
  0.0 273.3 jit_solution(11795213985586192007)
XLA Ops:
  7.2 0.0 copy-start
  7.2 0.0 copy-start.3
  7.2 0.0 all-gather.2.cloned.1.call-start
  7.3 0.8 convert_element_type.50
  8.1 0.8 iota_compare_fusion
  8.9 1.5 fusion.12
  10.4 0.7 convert_add_fusion.2
  11.1 0.7 convert_add_fusion.1
  11.8 2.2 fusion.37
  14.0 0.6 subtract_convert_fusion
  14.6 0.1 copy.17
  14.7 0.1 copy.16
  14.8 0.7 pad_maximum_fusion
  15.4 0.9 copy.19
  16.3 0.0 copy-done
  16.3 0.0 copy-done.3
  16.3 1.2 fusion.41
  17.6 5.8 %fusion.39 = f32[256,2048]{1,0:T(8,128)S(1)} fusion(bf16[2048,2048]{1,0:T(8,128)(2,1)} %param.19, bf16[256,2048]{1,0:T(8,128)(2,1)S(1)} %copy-done.3, f32[2048]{0:T(1024)S(1)} %convert_add_fusion.2, f32[256]{0:T(256)S(1)} %add_rsqrt_fusion.1), kind=kOutput, calls=%fused_computation.63 | convolution fusion | flops 2149580800 | bytes 11543552 | tf_op jit(solution)/shard_map/dot_general | solution.py:48
  23.3 0.0 copy-start.6
  23.3 0.9 copy.21
  24.2 0.2 multiply_subtract_fusion
  24.5 0.0 copy-done.6
  24.5 0.4 fusion.22
  24.9 25.8 %select_reduce_fusion = (f32[256,8]{1,0:T(8,128)S(1)}, f32[256,8,512]{2,1,0:T(8,128)S(1)}) fusion(pred[256,512]{1,0:T(8,128)(4,1)S(1)} %iota_compare_fusion, bf16[256,512,256]{2,1,0:T(8,128)(2,1)} %param.14, f32[256,8,128]{2,1,0:T(8,128)S(1)} %get-tuple-element.7, f32[256,8,128]{2,1,0:T(8,128)S(1)} %get-tuple-element.6), kind=kOutput, calls=%fused_computation.12 | convolution fusion | flops 540538880 | bytes 73539584 | tf_op jit(solution)/shard_map/bhd,btd->bht/dot_general | solution.py:28
  50.7 0.0 copy-start.2
  50.7 0.0 copy-start.5
  50.7 1.9 copy-done.2
  52.7 1.5 fusion.9
  54.2 0.0 copy-done.5
  54.3 25.0 %add_convert_fusion.1 = bf16[256,8,256]{2,1,0:T(8,128)(2,1)S(1)} fusion(bf16[256,512,256]{2,1,0:T(8,128)(2,1)} %param.15, f32[256,8,512]{2,1,0:T(8,128)} %copy-done.2, f32[256,8]{1,0:T(8,128)S(1)} %get-tuple-element.9, f32[256,8]{1,0:T(8,128)S(1)} %max.3, pred[256,512]{1,0:T(8,128)(4,1)S(1)} %iota_compare_fusion, f32[256,256]{1,0:T(8,128)S(1)} %copy-done.5, ...), kind=kOutput, calls=%fused_computation.27 | convolution fusion | flops 542638080 | bytes 72769536 | tf_op jit(solution)/shard_map/bht,btd->bhd/dot_general | solution.py:38
  79.2 0.3 copy.22
  79.5 6.1 %multiply_reduce_fusion = (f32[256]{0:T(256)S(1)}, f32[256,2048]{1,0:T(8,128)S(1)}) fusion(bf16[256,2048]{1,0:T(8,128)(2,1)S(1)} %bitcast.32, bf16[2048,2048]{1,0:T(8,128)(2,1)} %param.22, bf16[256,2048]{1,0:T(8,128)(2,1)} %param.13), kind=kOutput, calls=%fused_computation.26 | convolution fusion | flops 2149580544 | bytes 12583936 | tf_op jit(solution)/shard_map/dot_general | solution.py:55
  85.7 1.2 multiply_convert_fusion
  86.9 0.0 all-gather.2.cloned.1.call-update
  86.9 0.0 reduce-scatter.2.cloned.1.call-start
  87.0 34.4 %all-gather.2.cloned.1.call-done = bf16[1024,2048]{1,0:T(8,128)(2,1)} async-done(((bf16[256,2048]{1,0:T(8,128)(2,1)}), bf16[1024,2048]{1,0:T(8,128)(2,1)}) %all-gather.2.cloned.1.call-update) | async-done | bytes 4194320 | tf_op jit(solution)/shard_map/all_gather | solution.py:68
  121.4 0.0 copy-start.7
  121.4 24.3 %fusion.42 = f32[1024,4096]{1,0:T(8,128)} fusion(bf16[1024,2048]{1,0:T(8,128)(2,1)} %all-gather.2.cloned.1.call-done, bf16[2048,4096]{1,0:T(8,128)(2,1)} %param.23), kind=kOutput, calls=%fused_computation.65 | convolution fusion | flops 17179869184 | bytes 37748736 | tf_op jit(solution)/shard_map/dot_general | solution.py:69
  145.7 0.0 copy-done.7
  145.7 28.7 %fusion.8.clone.4 = bf16[1024,4096]{1,0:T(8,128)(2,1)} fusion(f32[1024,4096]{1,0:T(8,128)} %fusion.42, bf16[1024,2048]{1,0:T(8,128)(2,1)S(1)} %copy-done.7, bf16[2048,4096]{1,0:T(8,128)(2,1)} %param.24), kind=kOutput, calls=%fused_computation.9.clone.clone.clone.1 | convolution fusion | flops 17221812224 | bytes 46137344 | tf_op jit(solution)/shard_map/dot_general | solution.py:70
  174.4 24.0 %fusion.10 = f32[1024,2048]{1,0:T(8,128)} fusion(bf16[4096,2048]{1,0:T(8,128)(2,1)} %param.25, bf16[1024,4096]{1,0:T(8,128)(2,1)} %fusion.8.clone.4), kind=kOutput, calls=%fused_computation.17 | convolution fusion | flops 17179869184 | bytes 33554432 | tf_op jit(solution)/shard_map/dot_general | solution.py:72
  198.4 0.0 copy-start.4
  198.4 0.0 reduce-scatter.2.cloned.1.call-update
  198.4 0.0 copy-start.1
  198.4 0.9 copy-done.4
  199.3 0.8 copy.18
  200.0 63.6 %reduce-scatter.2.cloned.1.call-done = f32[256,2048]{1,0:T(8,128)} async-done(((f32[1024,2048]{1,0:T(8,128)}), f32[256,2048]{1,0:T(8,128)}) %reduce-scatter.2.cloned.1.call-update) | async-done | bytes 2097168 | tf_op jit(solution)/shard_map/reduce_scatter | solution.py:73
  263.7 2.8 %add_convert_fusion = bf16[256,2048]{1,0:T(8,128)(2,1)} fusion(f32[256,2048]{1,0:T(8,128)S(1)} %get-tuple-element.21, f32[256,2048]{1,0:T(8,128)} %reduce-scatter.2.cloned.1.call-done), kind=kLoop, calls=%fused_computation.24 | loop fusion | flops 1048576 | bytes 5242880 | tf_op jit(solution)/shard_map/convert_element_type | solution.py:74
  266.5 0.0 copy-done.1
  (5 shorter events, 0.1 us)
Async XLA Ops:
  7.2 9.2 %copy-start = (bf16[2048,256]{1,0:T(8,128)(2,1)S(1)}, bf16[2048,256]{1,0:T(8,128)(2,1)}, u32[]{:S(2)}) copy-start(bf16[2048,256]{1,0:T(8,128)(2,1)} %param.21) | copy-start | bytes 3145732
  7.2 9.1 %copy-start.3 = (bf16[256,2048]{1,0:T(8,128)(2,1)S(1)}, bf16[256,2048]{1,0:T(8,128)(2,1)}, u32[]{:S(2)}) copy-start(bf16[256,2048]{1,0:T(8,128)(2,1)} %param.13) | copy-start | bytes 3145732
  7.2 114.2 %all-gather.2.cloned.1.call-start = ((), (), s32[]{:S(2)}) async-start(), calls=%async_computation.1 | async-start | bytes 5242880 | tf_op jit(solution)/shard_map/all_gather | solution.py:68
  23.3 1.1 copy-start.6
  50.7 2.0 copy-start.2
  50.7 3.5 %copy-start.5 = (f32[256,256]{1,0:T(8,128)S(1)}, f32[256,256]{1,0:T(8,128)}, u32[]{:S(2)}) copy-start(f32[256,256]{1,0:T(8,128)} %get-tuple-element.18) | copy-start | bytes 786436
  86.9 176.7 %reduce-scatter.2.cloned.1.call-start = ((), (), s32[]{:S(2)}) async-start(), calls=%async_computation.2 | async-start | bytes 10485760 | tf_op jit(solution)/shard_map/reduce_scatter | solution.py:73
  121.4 24.3 %copy-start.7 = (bf16[1024,2048]{1,0:T(8,128)(2,1)S(1)}, bf16[1024,2048]{1,0:T(8,128)(2,1)}, u32[]{:S(2)}) copy-start(bf16[1024,2048]{1,0:T(8,128)(2,1)} %all-gather.2.cloned.1.call-done) | copy-start | bytes 12582916
  198.4 0.9 copy-start.4
  198.4 68.1 %copy-start.1 = (bf16[2048,256]{1,0:T(8,128)(2,1)S(1)}, bf16[2048,256]{1,0:T(8,128)(2,1)}, u32[]{:S(2)}) copy-start(bf16[2048,256]{1,0:T(8,128)(2,1)} %param.21) | copy-start | bytes 3145732
Sparse Core Ops, SparseCore 0:
  87.0 34.3 all-gather.1
  198.5 65.0 reduce-scatter.1
where the time goes:
time: 274 us; the launch traced here: 273 us
  matrix products  144 us (53%)
  waiting for transfers between devices  98.1 us (36%)
  between operations  14.2 us (5%)
  other arithmetic  11.6 us (4%)
  local copies, waits for them, and re-layouts  5.82 us (2%)
    reduce_scatter x1, waiting for transfers between devices, per_device(): down_sum = lax.psum_scatter(part_sum, 'tp', scatter_dimension=0, tiled=True)  63.6 us
    all_gather x1, waiting for transfers between devices, per_device(): group_rows = lax.all_gather(xn_mid, 'tp', axis=0, tiled=True)  34.4 us
    dot_general x1, matrix products, per_device(): up_act = jnp.dot(group_rows, w_up, preferred_element_type=jnp.float32)  28.7 us
    dot_general x1, matrix products, attend(): jnp.einsum('bhd,btd->bht', q_rot, k_cache, preferred_element_type=jnp.flo...  25.8 us
    dot_general x1, matrix products, attend(): jnp.einsum('bht,btd->bhd', hist_prob, v_cache, preferred_element_type=jnp...  25 us
    dot_general x1, matrix products, per_device(): gate_act = jnp.dot(group_rows, w_gate, preferred_element_type=jnp.float32)  24.3 us
    dot_general x1, matrix products, per_device(): part_sum = jnp.dot(hidden_act, w_down, preferred_element_type=jnp.float32)  24 us
    dot_general x1, matrix products, attention_block(): jnp.dot(attn_out.reshape(num_rows, num_heads * head_dim), w_o, preferred_...  6.12 us
  transfers between devices with their start and end apart: 2, of which 2 were waited for; matrix products, arithmetic and copies ran while one was open for 0% of the time, Pallas kernels for 0%

commit v1 on v0

--- a/solution.py
+++ b/solution.py
@@ -1,7 +1,15 @@
+import functools
+
 import jax
 import jax.numpy as jnp
 from jax import lax
+from jax.experimental import pallas as pl
+from jax.experimental.pallas import tpu as pltpu
 from jax.sharding import PartitionSpec as P
+
+GROUP = 8
+RING = 4
+GRAIN = 16
 
 
 def rms_scale(values, gain_vec):
@@ -24,20 +32,110 @@
     return jnp.concatenate([first_half * cos_t - second_half * sin_t, second_half * cos_t + first_half * sin_t], axis=-1)
 
 
+def attend_kernel(num_groups, len_ref, q_ref, kn_ref, vn_ref, k_hbm, v_hbm, o_ref,
+                  k_buf, v_buf, s_buf, k_sem, v_sem):
+    cap = k_buf.shape[1]
+
+    def copy(src_hbm, dst_buf, sems, group, lane):
+        row = group * GROUP + lane
+        slot = lax.rem(group, RING) * GROUP + lane
+        used = pl.multiple_of((len_ref[row] + (GRAIN - 1)) // GRAIN * GRAIN, GRAIN)
+        return pltpu.make_async_copy(src_hbm.at[row, pl.ds(0, used), :],
+                                     dst_buf.at[slot, pl.ds(0, used), :], sems.at[slot])
+
+    def start(src_hbm, dst_buf, sems, group):
+        for lane in range(GROUP):
+            copy(src_hbm, dst_buf, sems, group, lane).start()
+
+    def wait(src_hbm, dst_buf, sems, group):
+        for lane in range(GROUP):
+            copy(src_hbm, dst_buf, sems, group, lane).wait()
+
+    def scores(group):
+        base = lax.rem(group, RING) * GROUP
+        for lane in range(GROUP):
+            s_buf[lax.rem(group, 2), lane] = lax.dot_general(
+                q_ref[group * GROUP + lane], k_buf[base + lane],
+                (((1,), (1,)), ((), ())), preferred_element_type=jnp.float32)
+
+    def outputs(group):
+        base = lax.rem(group, RING) * GROUP
+        first = pl.multiple_of(group * GROUP, GROUP)
+        k_new = kn_ref[pl.ds(first, GROUP), :]
+        v_new = vn_ref[pl.ds(first, GROUP), :]
+        place = lax.broadcasted_iota(jnp.int32, (GROUP, cap), 1)
+        for lane in range(GROUP):
+            row = first + lane
+            score = jnp.where(place < len_ref[row], s_buf[lax.rem(group, 2), lane], -jnp.inf)
+            q_wide = q_ref[row].astype(jnp.float32)
+            new_score = jnp.sum(q_wide * k_new[lane:lane + 1, :], axis=-1, keepdims=True)
+            peak = jnp.maximum(jnp.max(score, axis=-1, keepdims=True), new_score)
+            weight = jnp.exp(score - peak)
+            new_weight = jnp.exp(new_score - peak)
+            scale = 1.0 / (jnp.sum(weight, axis=-1, keepdims=True) + new_weight)
+            prob = (weight * scale).astype(jnp.bfloat16)
+            new_prob = (new_weight * scale).astype(jnp.bfloat16).astype(jnp.float32)
+            mixed = jnp.dot(prob, v_buf[base + lane], preferred_element_type=jnp.float32)
+            o_ref[row] = (mixed + new_prob * v_new[lane:lane + 1, :]).astype(jnp.bfloat16)
+
+    for group in range(RING):
+        start(k_hbm, k_buf, k_sem, group)
+
+    def clear(slot, carry):
+        v_buf[slot] = jnp.zeros(v_buf.shape[1:], v_buf.dtype)
+        return carry
+
+    lax.fori_loop(0, v_buf.shape[0], clear, 0)
+    for group in range(RING):
+        start(v_hbm, v_buf, v_sem, group)
+
+    wait(k_hbm, k_buf, k_sem, 0)
+    scores(0)
+    start(k_hbm, k_buf, k_sem, RING)
+
+    def step(group, carry):
+        wait(k_hbm, k_buf, k_sem, group + 1)
+        wait(v_hbm, v_buf, v_sem, group)
+        scores(group + 1)
+        outputs(group)
+
+        @pl.when(group + 1 + RING < num_groups)
+        def _():
+            start(k_hbm, k_buf, k_sem, group + 1 + RING)
+
+        @pl.when(group + RING < num_groups)
+        def _():
+            start(v_hbm, v_buf, v_sem, group + RING)
+        return carry
+
+    lax.fori_loop(0, num_groups - 1, step, 0)
+    wait(v_hbm, v_buf, v_sem, num_groups - 1)
+    outputs(num_groups - 1)
+
+
 def attend(q_rot, k_new, v_new, k_cache, v_cache, cache_len):
-    hist_score = jnp.einsum('bhd,btd->bht', q_rot, k_cache, preferred_element_type=jnp.float32)
-    new_score = jnp.einsum('bhd,bd->bh', q_rot, k_new, preferred_element_type=jnp.float32)
-    valid_mask = lax.broadcasted_iota(jnp.int32, (1, 1, k_cache.shape[1]), 2) < cache_len[:, None, None]
-    hist_score = jnp.where(valid_mask, hist_score, -jnp.inf)
-    peak_score = jnp.maximum(jnp.max(hist_score, axis=-1), new_score)
-    hist_weight = jnp.exp(hist_score - peak_score[..., None])
-    new_weight = jnp.exp(new_score - peak_score)
-    weight_sum = jnp.sum(hist_weight, axis=-1) + new_weight
-    hist_prob = (hist_weight / weight_sum[..., None]).astype(jnp.bfloat16)
-    new_prob = (new_weight / weight_sum).astype(jnp.bfloat16)
-    attn_out = jnp.einsum('bht,btd->bhd', hist_prob, v_cache, preferred_element_type=jnp.float32)
-    attn_out = attn_out + new_prob.astype(jnp.float32)[..., None] * v_new.astype(jnp.float32)[:, None, :]
-    return attn_out.astype(jnp.bfloat16)
+    rows, heads, dim = q_rot.shape
+    cap = k_cache.shape[1]
+    vmem = pl.BlockSpec(memory_space=pltpu.VMEM)
+    hbm = pl.BlockSpec(memory_space=pl.ANY)
+    return pl.pallas_call(
+        functools.partial(attend_kernel, rows // GROUP),
+        name='attend',
+        out_shape=jax.ShapeDtypeStruct((rows, heads, dim), jnp.bfloat16),
+        in_specs=[pl.BlockSpec(memory_space=pltpu.SMEM), vmem, vmem, vmem, hbm, hbm],
+        out_specs=vmem,
+        scratch_shapes=[
+            pltpu.VMEM((RING * GROUP, cap, dim), jnp.bfloat16),
+            pltpu.VMEM((RING * GROUP, cap, dim), jnp.bfloat16),
+            pltpu.VMEM((2, GROUP, heads, cap), jnp.float32),
+            pltpu.SemaphoreType.DMA((RING * GROUP,)),
+            pltpu.SemaphoreType.DMA((RING * GROUP,)),
+        ],
+        compiler_params=pltpu.CompilerParams(vmem_limit_bytes=40 * 1024 * 1024),
+        cost_estimate=pl.CostEstimate(flops=4 * rows * heads * dim * cap,
+                                      bytes_accessed=2 * rows * cap * dim * 2,
+                                      transcendentals=rows * heads * cap),
+    )(cache_len, q_rot, k_new.astype(jnp.float32), v_new.astype(jnp.float32), k_cache, v_cache)
 
 
 def attention_block(hidden_in, k_cache, v_cache, cache_len, norm_attn, w_q, w_k, w_v, w_o):

time: 274 us -> 257 us (0.938)
  matrix products: 144 us -> 90.1 us
  Pallas kernels: 0 us -> 42.3 us
  local copies, waits for them, and re-layouts: 5.82 us -> 1.22 us
    dot_general x3 -> x0, matrix products: 51.2 us -> none  [the longest x1 25.8 us: attend(): jnp.einsum('bhd,btd->bht', q_rot, k_cache, preferred_element_type=jnp.flo...]
    pallas_call x0 -> x1, Pallas kernels: none -> 42.3 us  [attend(): pl.pallas_call(functools.partial(attend_kernel, rows // GROUP), name='att...]
    dot_general x1, matrix products: 6.12 us -> 2.57 us  [attention_block(): jnp.dot(attn_out.reshape(num_rows, num_heads * head_dim), w_o, preferred_...]
    unnamed x19 -> x16, local copies, waits for them, and re-layouts: 4.77 us -> 1.22 us
where the time goes in v1:
time: 257 us
  waiting for transfers between devices  99.3 us (39%)
  matrix products  90.1 us (35%)
  Pallas kernels  42.3 us (16%)
  between operations  14.2 us (6%)
  other arithmetic  9.41 us (4%)
    reduce_scatter x1, waiting for transfers between devices, per_device(): down_sum = lax.psum_scatter(part_sum, 'tp', scatter_dimension=0, tiled=True)  65.2 us
    pallas_call x1, Pallas kernels, attend(): pl.pallas_call(functools.partial(attend_kernel, rows // GROUP), name='att...  42.3 us
    all_gather x1, waiting for transfers between devices, per_device(): group_rows = lax.all_gather(xn_mid, 'tp', axis=0, tiled=True)  34 us
    dot_general x1, matrix products, per_device(): up_act = jnp.dot(group_rows, w_up, preferred_element_type=jnp.float32)  28.7 us
    dot_general x1, matrix products, per_device(): gate_act = jnp.dot(group_rows, w_gate, preferred_element_type=jnp.float32)  24.2 us
    dot_general x1, matrix products, per_device(): part_sum = jnp.dot(hidden_act, w_down, preferred_element_type=jnp.float32)  24.1 us
    dot_general x1, matrix products, attention_block(): jnp.dot(normed, w_q, preferred_element_type=jnp.float32)  6.09 us
  transfers between devices with their start and end apart: 2, of which 2 were waited for; matrix products, arithmetic and copies ran while one was open for 0% of the time, Pallas kernels for 0%

profile of v1, /device:TPU:0, one launch (start us, length us, event | category | flops | bytes accessed | tf_op | source)
XLA Modules:
  0.0 256.8 jit_solution(14496928012494282282)
XLA Ops:
  7.2 0.0 copy-start
  7.2 0.0 all-gather.2.cloned.1.call-start
  7.2 0.8 convert_element_type.41
  8.0 1.5 fusion.10
  9.5 0.7 convert_add_fusion.2
  10.2 0.7 convert_add_fusion.1
  10.9 2.0 fusion.19
  12.9 0.0 copy-done
  13.0 2.4 fusion.24
  15.3 6.1 %fusion.21 = f32[256,2048]{1,0:T(8,128)S(1)} fusion(bf16[2048,2048]{1,0:T(8,128)(2,1)} %param.19, bf16[256,2048]{1,0:T(8,128)(2,1)} %param.13, f32[2048]{0:T(1024)S(1)} %convert_add_fusion.2, f32[256]{0:T(256)S(1)} %add_rsqrt_fusion.1), kind=kOutput, calls=%fused_computation.40 | convolution fusion | flops 2149580800 | bytes 11543552 | tf_op jit(solution)/shard_map/dot_general | solution.py:146
  21.4 0.0 copy-start.2
  21.4 0.9 copy.19
  22.3 0.6 subtract_convert_fusion
  22.9 0.7 fusion.23
  23.6 0.3 multiply_subtract_fusion
  23.9 0.0 slice-start
  23.9 0.2 fusion.13.q_ref
  24.1 0.0 copy-done.2
  24.1 0.0 copy-start.3
  24.1 0.0 slice-start.1
  24.1 42.3 %attend.1 = bf16[256,8,256]{2,1,0:T(8,128)(2,1)S(1)} custom-call(s32[256]{0:T(256)S(1)} %copy-done.2, bf16[256,8,256]{2,1,0:T(8,128)(2,1)S(1)} %fusion.13.q_ref, f32[256,256]{1,0:T(8,128)S(1)} %get-tuple-element.3.kn_ref, f32[256,256]{1,0:T(8,128)S(1)} %get-tuple-element.11.vn_ref, bf16[256,512,256]{2,1,0:T(8,128)(2,1)} %k_hbm.1, bf16[256,512,256]{2,1,0:T(8,128)(2,1)} %v_hbm.1), custom_call_target="tpu_custom_call" | custom-call | flops 1073741824 | bytes 134217728 | tf_op jit(solution)/shard_map/attend/pallas_call | solution.py:121
  66.4 0.3 copy.20
  66.8 0.0 slice-done
  66.8 0.0 copy-done.3
  66.8 0.0 slice-done.1
  66.8 2.6 %multiply_reduce_fusion = (f32[256]{0:T(256)S(1)}, f32[256,2048]{1,0:T(8,128)S(1)}) fusion(bf16[256,2048]{1,0:T(8,128)(2,1)S(1)} %bitcast.25, bf16[2048,2048]{1,0:T(8,128)(2,1)S(1)} %bitcast.27, bf16[256,2048]{1,0:T(8,128)(2,1)S(1)} %copy-done.3), kind=kOutput, calls=%fused_computation.21 | convolution fusion | flops 2149580544 | bytes 12583936 | tf_op jit(solution)/shard_map/dot_general | solution.py:153
  69.4 1.2 multiply_convert_fusion
  70.6 0.0 all-gather.2.cloned.1.call-update
  70.6 0.2 reduce-scatter.2.cloned.1.call-start
  70.9 34.0 %all-gather.2.cloned.1.call-done = bf16[1024,2048]{1,0:T(8,128)(2,1)} async-done(((bf16[256,2048]{1,0:T(8,128)(2,1)}), bf16[1024,2048]{1,0:T(8,128)(2,1)}) %all-gather.2.cloned.1.call-update) | async-done | bytes 4194320 | tf_op jit(solution)/shard_map/all_gather | solution.py:166
  104.9 0.0 copy-start.4
  104.9 24.2 %fusion.25 = f32[1024,4096]{1,0:T(8,128)} fusion(bf16[1024,2048]{1,0:T(8,128)(2,1)} %all-gather.2.cloned.1.call-done, bf16[2048,4096]{1,0:T(8,128)(2,1)} %param.23), kind=kOutput, calls=%fused_computation.43 | convolution fusion | flops 17179869184 | bytes 37748736 | tf_op jit(solution)/shard_map/dot_general | solution.py:167
  129.1 0.0 copy-done.4
  129.1 28.7 %fusion.8.clone.4 = bf16[1024,4096]{1,0:T(8,128)(2,1)} fusion(f32[1024,4096]{1,0:T(8,128)} %fusion.25, bf16[1024,2048]{1,0:T(8,128)(2,1)S(1)} %copy-done.4, bf16[2048,4096]{1,0:T(8,128)(2,1)} %param.24), kind=kOutput, calls=%fused_computation.9.clone.clone.clone.1 | convolution fusion | flops 17221812224 | bytes 46137344 | tf_op jit(solution)/shard_map/dot_general | solution.py:168
  157.8 0.0 copy-start.1
  157.8 24.1 %fusion.9 = f32[1024,2048]{1,0:T(8,128)} fusion(bf16[4096,2048]{1,0:T(8,128)(2,1)} %param.25, bf16[1024,4096]{1,0:T(8,128)(2,1)} %fusion.8.clone.4), kind=kOutput, calls=%fused_computation.13 | convolution fusion | flops 17179869184 | bytes 33554432 | tf_op jit(solution)/shard_map/dot_general | solution.py:170
  181.9 0.0 reduce-scatter.2.cloned.1.call-update
  181.9 65.2 %reduce-scatter.2.cloned.1.call-done = f32[256,2048]{1,0:T(8,128)} async-done(((f32[1024,2048]{1,0:T(8,128)}), f32[256,2048]{1,0:T(8,128)}) %reduce-scatter.2.cloned.1.call-update) | async-done | bytes 2097168 | tf_op jit(solution)/shard_map/reduce_scatter | solution.py:171
  247.2 2.8 %add_convert_fusion = bf16[256,2048]{1,0:T(8,128)(2,1)} fusion(f32[256,2048]{1,0:T(8,128)S(1)} %get-tuple-element.14, f32[256,2048]{1,0:T(8,128)} %reduce-scatter.2.cloned.1.call-done), kind=kLoop, calls=%fused_computation.19 | loop fusion | flops 1048576 | bytes 5242880 | tf_op jit(solution)/shard_map/convert_element_type | solution.py:172
  250.0 0.0 copy-done.1
  (4 shorter events, 0.0 us)
Async XLA Ops:
  7.2 5.8 %copy-start = (bf16[2048,256]{1,0:T(8,128)(2,1)S(1)}, bf16[2048,256]{1,0:T(8,128)(2,1)}, u32[]{:S(2)}) copy-start(bf16[2048,256]{1,0:T(8,128)(2,1)} %param.21) | copy-start | bytes 3145732
  7.2 97.7 %all-gather.2.cloned.1.call-start = ((), (), s32[]{:S(2)}) async-start(), calls=%async_computation.1 | async-start | bytes 5242880 | tf_op jit(solution)/shard_map/all_gather | solution.py:166
  21.4 2.6 %copy-start.2 = (s32[256]{0:T(256)S(1)}, s32[256]{0:T(256)}, u32[]{:S(2)}) copy-start(s32[256]{0:T(256)} %len_ref.1) | copy-start | bytes 3076
  23.9 42.9 %slice-start = ((s8[8388608]{0:T(1024)(128)(4,1)}), s8[4194304]{0:T(1024)(128)(4,1)S(1)}, s32[]{:S(2)}) async-start(s8[8388608]{0:T(1024)(128)(4,1)} %bitcast.26), calls=%async_computation.3 | async-start | bytes 8388608
  24.1 42.7 %copy-start.3 = (bf16[256,2048]{1,0:T(8,128)(2,1)S(1)}, bf16[256,2048]{1,0:T(8,128)(2,1)}, u32[]{:S(2)}) copy-start(bf16[256,2048]{1,0:T(8,128)(2,1)} %param.13) | copy-start | bytes 3145732
  24.1 42.7 %slice-start.1 = ((s8[8388608]{0:T(1024)(128)(4,1)}), s8[4194304]{0:T(1024)(128)(4,1)S(1)}, s32[]{:S(2)}) async-start(s8[8388608]{0:T(1024)(128)(4,1)} %bitcast.26), calls=%async_computation.4 | async-start | bytes 8388608
  70.6 176.5 %reduce-scatter.2.cloned.1.call-start = ((), (), s32[]{:S(2)}) async-start(), calls=%async_computation.2 | async-start | bytes 10485760 | tf_op jit(solution)/shard_map/reduce_scatter | solution.py:171
  104.9 24.2 %copy-start.4 = (bf16[1024,2048]{1,0:T(8,128)(2,1)S(1)}, bf16[1024,2048]{1,0:T(8,128)(2,1)}, u32[]{:S(2)}) copy-start(bf16[1024,2048]{1,0:T(8,128)(2,1)} %all-gather.2.cloned.1.call-done) | copy-start | bytes 12582916
  157.8 92.2 %copy-start.1 = (bf16[2048,256]{1,0:T(8,128)(2,1)S(1)}, bf16[2048,256]{1,0:T(8,128)(2,1)}, u32[]{:S(2)}) copy-start(bf16[2048,256]{1,0:T(8,128)(2,1)} %param.21) | copy-start | bytes 3145732
Sparse Core Ops, SparseCore 0:
  70.7 34.0 all-gather.1
  182.1 65.0 reduce-scatter.1

commit v2 on v1

--- a/solution.py
+++ b/solution.py
@@ -154,6 +154,221 @@
     return hidden_in.astype(jnp.float32) + mixed, k_new, v_new
 
 
+HID_BLOCK = 512
+OUT_BLOCK = 512
+WEIGHT_RING = 3
+MESH = pl.DeviceIdType.MESH
+
+
+def mlp_kernel(xn_ref, xmid_ref, wg_hbm, wu_hbm, wd_hbm, out_ref,
+               x_all, h_buf, g_buf, u_buf, wg_buf, wu_buf, wd_buf, acc_buf,
+               d_send, d_recv, c_send, c_recv, p_send, p_recv,
+               w_sem, wd_sem, send_sem, recv_sem):
+    rows, width = xn_ref.shape
+    half = rows // 2
+    hidden = wg_hbm.shape[1]
+    num_hid = hidden // HID_BLOCK
+    num_out = width // OUT_BLOCK
+    num_steps = 4 * num_hid
+    me = lax.axis_index('tp')
+    partner = me + 1 - 2 * lax.rem(me, 2)
+    counter = lax.rem(me + 2, 4)
+
+    barrier = pltpu.get_barrier_semaphore()
+    for peer in (partner, counter):
+        pl.semaphore_signal(barrier, inc=1, device_id={'tp': peer}, device_id_type=MESH)
+
+    def weight_copies(step):
+        slot = lax.rem(step, WEIGHT_RING)
+        cols = pl.ds(pl.multiple_of(lax.rem(step, num_hid) * HID_BLOCK, HID_BLOCK), HID_BLOCK)
+        return (pltpu.make_async_copy(wg_hbm.at[:, cols], wg_buf.at[slot], w_sem.at[slot, 0]),
+                pltpu.make_async_copy(wu_hbm.at[:, cols], wu_buf.at[slot], w_sem.at[slot, 1]))
+
+    def down_copy(block):
+        return pltpu.make_async_copy(wd_hbm.at[:, pl.ds(block * OUT_BLOCK, OUT_BLOCK)],
+                                     wd_buf.at[block], wd_sem.at[block])
+
+    def remote(src, dst, index, peer):
+        return pltpu.make_async_remote_copy(
+            src_ref=src, dst_ref=dst, send_sem=send_sem.at[index], recv_sem=recv_sem.at[index],
+            device_id={'tp': peer}, device_id_type=MESH)
+
+    gather_partner = remote(xn_ref, x_all.at[0], 0, partner)
+    gather_counter = [remote(xn_ref.at[pl.ds(i * half, half), :], x_all.at[1 + i, pl.ds(0, half), :], 1 + i, counter)
+                      for i in range(2)]
+    forward = [remote(x_all.at[1 + i, pl.ds(0, half), :], x_all.at[1 + i, pl.ds(half, half), :], 3 + i, partner)
+               for i in range(2)]
+
+    def cross(i, n):
+        return remote(d_send.at[i, n], d_recv.at[i, n], 5 + i * num_out + n, partner)
+
+    def home(i, n):
+        return remote(c_send.at[i, n], c_recv.at[i, n], 5 + (2 + i) * num_out + n, counter)
+
+    def side(n):
+        return remote(p_send.at[n], p_recv.at[n], 5 + 4 * num_out + n, partner)
+
+    for step in range(WEIGHT_RING):
+        for copy in weight_copies(step):
+            copy.start()
+    for block in range(num_out):
+        down_copy(block).start()
+    pl.semaphore_wait(barrier, 2)
+    gather_partner.start()
+    for copy in gather_counter:
+        copy.start()
+
+    def hidden_dots(x_ref, step):
+        slot = lax.rem(step, WEIGHT_RING)
+        keep = lax.rem(step, 2)
+        g_buf[keep] = jnp.dot(x_ref[...], wg_buf[slot], preferred_element_type=jnp.float32)
+        u_buf[keep] = jnp.dot(x_ref[...], wu_buf[slot], preferred_element_type=jnp.float32)
+
+    def activate(step, block):
+        keep = lax.rem(step, 2)
+        cols = pl.ds(pl.multiple_of(block * HID_BLOCK, HID_BLOCK), HID_BLOCK)
+        h_buf[:, cols] = (jax.nn.gelu(g_buf[keep], approximate=True) * u_buf[keep]).astype(jnp.bfloat16)
+
+    def prefetch(step):
+        @pl.when(step + WEIGHT_RING < num_steps)
+        def _():
+            for copy in weight_copies(step + WEIGHT_RING):
+                copy.start()
+
+    def hidden_phase(number, x_ref):
+        first = number * num_hid
+        for copy in weight_copies(first):
+            copy.wait()
+        hidden_dots(x_ref, first)
+        prefetch(first)
+
+        def body(block, carry):
+            step = first + block
+            for copy in weight_copies(step):
+                copy.wait()
+            hidden_dots(x_ref, step)
+            activate(step - 1, block - 1)
+            prefetch(step)
+            return carry
+
+        lax.fori_loop(1, num_hid, body, 0)
+        activate(first + num_hid - 1, num_hid - 1)
+
+    def down(n):
+        return jnp.dot(h_buf[...], wd_buf[n], preferred_element_type=jnp.float32)
+
+    gather_partner.wait_recv()
+    hidden_phase(0, x_all.at[0])
+    for n in range(num_out):
+        down_copy(n).wait()
+        p_send[n] = down(n)
+        side(n).start()
+    gather_counter[0].wait_recv()
+    forward[0].start()
+
+    for i in range(2):
+        forward[i].wait_recv()
+        hidden_phase(1 + i, x_all.at[1 + i])
+        if i == 0:
+            gather_counter[1].wait_recv()
+            forward[1].start()
+
+        def finish(n, i=i):
+            cross(i, n).wait_recv()
+            c_send[i, n] = c_send[i, n] + d_recv[i, n]
+            home(i, n).start()
+
+        def body(n, carry, i=i):
+            part = down(n)
+            c_send[i, n] = part[:half]
+            d_send[i, n] = part[half:]
+            cross(i, n).start()
+
+            @pl.when(n > 0)
+            def _():
+                finish(n - 1)
+            return carry
+
+        lax.fori_loop(0, num_out, body, 0)
+        finish(num_out - 1)
+
+    hidden_phase(3, xn_ref)
+
+    def own(n, carry):
+        acc_buf[n] = down(n)
+        return carry
+
+    lax.fori_loop(0, num_out, own, 0)
+
+    def settle(n, carry):
+        cols = pl.ds(pl.multiple_of(n * OUT_BLOCK, OUT_BLOCK), OUT_BLOCK)
+        side(n).wait_recv()
+        for i in range(2):
+            part = pl.ds(i * half, half)
+            home(i, n).wait_recv()
+            total = acc_buf[n, part, :] + p_recv[n, part, :] + c_recv[i, n]
+            out_ref[part, cols] = (xmid_ref[part, cols] + total).astype(jnp.bfloat16)
+        return carry
+
+    lax.fori_loop(0, num_out, settle, 0)
+
+    gather_partner.wait_send()
+    for i in range(2):
+        gather_counter[i].wait_send()
+        forward[i].wait_send()
+
+    def drain(n, carry):
+        side(n).wait_send()
+        for i in range(2):
+            cross(i, n).wait_send()
+            home(i, n).wait_send()
+        return carry
+
+    lax.fori_loop(0, num_out, drain, 0)
+
+
+def mlp_block(xn_mid, x_mid, w_gate, w_up, w_down):
+    rows, width = xn_mid.shape
+    half = rows // 2
+    hidden = w_gate.shape[1]
+    num_out = width // OUT_BLOCK
+    num_copies = 5 + 5 * num_out
+    vmem = pl.BlockSpec(memory_space=pltpu.VMEM)
+    hbm = pl.BlockSpec(memory_space=pl.ANY)
+    return pl.pallas_call(
+        mlp_kernel,
+        name='mlp',
+        out_shape=jax.ShapeDtypeStruct((rows, width), jnp.bfloat16),
+        in_specs=[vmem, vmem, hbm, hbm, hbm],
+        out_specs=vmem,
+        scratch_shapes=[
+            pltpu.VMEM((3, rows, width), jnp.bfloat16),
+            pltpu.VMEM((rows, hidden), jnp.bfloat16),
+            pltpu.VMEM((2, rows, HID_BLOCK), jnp.float32),
+            pltpu.VMEM((2, rows, HID_BLOCK), jnp.float32),
+            pltpu.VMEM((WEIGHT_RING, width, HID_BLOCK), jnp.bfloat16),
+            pltpu.VMEM((WEIGHT_RING, width, HID_BLOCK), jnp.bfloat16),
+            pltpu.VMEM((num_out, hidden, OUT_BLOCK), jnp.bfloat16),
+            pltpu.VMEM((num_out, rows, OUT_BLOCK), jnp.float32),
+            pltpu.VMEM((2, num_out, half, OUT_BLOCK), jnp.float32),
+            pltpu.VMEM((2, num_out, half, OUT_BLOCK), jnp.float32),
+            pltpu.VMEM((2, num_out, half, OUT_BLOCK), jnp.float32),
+            pltpu.VMEM((2, num_out, half, OUT_BLOCK), jnp.float32),
+            pltpu.VMEM((num_out, rows, OUT_BLOCK), jnp.float32),
+            pltpu.VMEM((num_out, rows, OUT_BLOCK), jnp.float32),
+            pltpu.SemaphoreType.DMA((WEIGHT_RING, 2)),
+            pltpu.SemaphoreType.DMA((num_out,)),
+            pltpu.SemaphoreType.DMA((num_copies,)),
+            pltpu.SemaphoreType.DMA((num_copies,)),
+        ],
+        compiler_params=pltpu.CompilerParams(collective_id=0, has_side_effects=True,
+                                             vmem_limit_bytes=62 * 1024 * 1024),
+        cost_estimate=pl.CostEstimate(flops=24 * rows * width * hidden,
+                                      bytes_accessed=9 * width * hidden * 2,
+                                      transcendentals=4 * rows * hidden),
+    )(xn_mid, x_mid, w_gate, w_up, w_down)
+
+
 def solution(mesh):
     row_spec = P(('dp', 'tp'), None)
     cache_spec = P(('dp', 'tp'), None, None)
@@ -163,13 +378,8 @@
     def per_device(hidden_in, k_cache, v_cache, cache_len, norm_attn, norm_mlp, w_q, w_k, w_v, w_o, w_gate, w_up, w_down):
         x_mid, k_new, v_new = attention_block(hidden_in, k_cache, v_cache, cache_len, norm_attn, w_q, w_k, w_v, w_o)
         xn_mid = rms_scale(x_mid, norm_mlp)
-        group_rows = lax.all_gather(xn_mid, 'tp', axis=0, tiled=True)
-        gate_act = jnp.dot(group_rows, w_gate, preferred_element_type=jnp.float32)
-        up_act = jnp.dot(group_rows, w_up, preferred_element_type=jnp.float32)
-        hidden_act = (jax.nn.gelu(gate_act, approximate=True) * up_act).astype(jnp.bfloat16)
-        part_sum = jnp.dot(hidden_act, w_down, preferred_element_type=jnp.float32)
-        down_sum = lax.psum_scatter(part_sum, 'tp', scatter_dimension=0, tiled=True)
-        return (x_mid + down_sum).astype(jnp.bfloat16), k_new, v_new
+        hidden_out = mlp_block(xn_mid, x_mid, w_gate, w_up, w_down)
+        return hidden_out, k_new, v_new
 
     return jax.shard_map(
         per_device,

time: 257 us -> 156 us (0.61)
  waiting for transfers between devices: 99.3 us -> 0 us
  Pallas kernels: 42.3 us -> 134 us
  matrix products: 90.1 us -> 11.6 us
  between operations: 14.2 us -> 0.8 us
  other arithmetic: 9.41 us -> 5.27 us
  local copies, waits for them, and re-layouts: 1.22 us -> 4.82 us
    pallas_call x0 -> x1, Pallas kernels: none -> 92 us  [mlp_block(): pl.pallas_call(mlp_kernel, name='mlp', out_shape=jax.ShapeDtypeStruct((ro...]
    dot_general x3 -> x0, matrix products: 77 us -> none  [the longest x1 28.7 us: per_device(): up_act = jnp.dot(group_rows, w_up, preferred_element_type=jnp.float32)]
    reduce_scatter x1 -> x0, waiting for transfers between devices: 65.2 us -> none  [per_device(): down_sum = lax.psum_scatter(part_sum, 'tp', scatter_dimension=0, tiled=True)]
    all_gather x1 -> x0, waiting for transfers between devices: 34 us -> none  [per_device(): group_rows = lax.all_gather(xn_mid, 'tp', axis=0, tiled=True)]
    unnamed x16 -> x19, local copies, waits for them, and re-layouts: 1.22 us -> 4.82 us
    convert_element_type x1 -> x0, other arithmetic: 2.8 us -> none  [per_device(): return ((x_mid + down_sum).astype(jnp.bfloat16), k_new, v_new)]
  transfers between devices with their start and end apart: 2 -> 0, of which waited for: 2 -> 0; matrix products, arithmetic and copies ran while one was open for 0% -> 0% of each run, Pallas kernels for 0% -> 0%
where the time goes in v2:
time: 156 us; the launch traced here: 157 us
  Pallas kernels  134 us (86%)
  matrix products  11.6 us (7%)
  other arithmetic  5.27 us (3%)
  local copies, waits for them, and re-layouts  4.82 us (3%)
    pallas_call x1, Pallas kernels, mlp_block(): pl.pallas_call(mlp_kernel, name='mlp', out_shape=jax.ShapeDtypeStruct((ro...  92 us
    pallas_call x1, Pallas kernels, attend(): pl.pallas_call(functools.partial(attend_kernel, rows // GROUP), name='att...  42.1 us
    dot_general x1, matrix products, attention_block(): jnp.dot(normed, w_q, preferred_element_type=jnp.float32)  5.77 us
    unnamed x19, local copies, waits for them, and re-layouts  4.82 us

profile of v2, /device:TPU:0, one launch (start us, length us, event | category | flops | bytes accessed | tf_op | source)
XLA Modules:
  0.0 156.7 jit_solution(14856248702991810763)
XLA Ops:
  0.6 0.0 copy-start
  0.6 0.8 convert_add_fusion.2
  1.4 0.0 copy-start.2
  1.4 1.5 fusion
  3.0 0.0 copy-start.4
  3.0 2.1 %fusion.5 = f32[256,256]{1,0:T(8,128)S(1)} fusion(bf16[2048,256]{1,0:T(8,128)(2,1)} %param.20, bf16[256,2048]{1,0:T(8,128)(2,1)} %param.13, f32[2048]{0:T(1024)S(1)} %convert_add_fusion.2, f32[256]{0:T(256)S(1)} %add_rsqrt_fusion.1), kind=kOutput, calls=%fused_computation.23 | convolution fusion | flops 270532608 | bytes 2368512 | tf_op jit(solution)/shard_map/dot_general | solution.py:147
  5.1 0.0 copy-done.2
  5.1 0.6 subtract_convert_fusion
  5.7 0.0 copy-done.4
  5.7 5.8 %fusion.7 = f32[256,2048]{1,0:T(8,128)S(1)} fusion(bf16[2048,2048]{1,0:T(8,128)(2,1)} %param.19, bf16[256,2048]{1,0:T(8,128)(2,1)S(1)} %copy-done.4, f32[2048]{0:T(1024)S(1)} %convert_add_fusion.2, f32[256]{0:T(256)S(1)} %add_rsqrt_fusion.1), kind=kOutput, calls=%fused_computation.24 | convolution fusion | flops 2149580800 | bytes 11543552 | tf_op jit(solution)/shard_map/dot_general | solution.py:146
  11.5 0.9 copy.19
  12.4 0.3 multiply_subtract_fusion
  12.7 0.2 fusion.3.q_ref
  12.9 0.7 fusion.9
  13.5 0.0 copy-done
  13.6 0.0 slice-start
  13.6 1.2 fusion.10
  14.7 0.0 slice-start.1
  14.7 42.1 %attend.1 = bf16[256,8,256]{2,1,0:T(8,128)(2,1)S(1)} custom-call(s32[256]{0:T(256)S(1)} %copy-done.2, bf16[256,8,256]{2,1,0:T(8,128)(2,1)S(1)} %fusion.3.q_ref, f32[256,256]{1,0:T(8,128)S(1)} %get-tuple-element.3.kn_ref, f32[256,256]{1,0:T(8,128)S(1)} %get-tuple-element.11.vn_ref, bf16[256,512,256]{2,1,0:T(8,128)(2,1)} %k_hbm.1, bf16[256,512,256]{2,1,0:T(8,128)(2,1)} %v_hbm.1), custom_call_target="tpu_custom_call" | custom-call | flops 1073741824 | bytes 134217728 | tf_op jit(solution)/shard_map/attend/pallas_call | solution.py:121
  56.9 0.3 copy.20
  57.2 0.0 slice-done
  57.2 0.0 slice-done.1
  57.2 0.0 copy-start.5
  57.2 2.6 %multiply_reduce_fusion = (f32[256]{0:T(256)S(1)}, f32[256,2048]{1,0:T(8,128)S(1)}) fusion(bf16[256,2048]{1,0:T(8,128)(2,1)S(1)} %bitcast.12, bf16[2048,2048]{1,0:T(8,128)(2,1)S(1)} %bitcast.14, bf16[256,2048]{1,0:T(8,128)(2,1)S(1)} %copy-done.4), kind=kOutput, calls=%fused_computation.9 | convolution fusion | flops 2149580544 | bytes 12583936 | tf_op jit(solution)/shard_map/dot_general | solution.py:153
  59.8 0.0 copy-start.3
  59.8 0.0 copy-done.5
  59.8 1.3 copy-done.3
  61.2 1.2 multiply_convert_fusion.xn_ref
  62.4 0.0 copy-start.1
  62.4 92.0 %mlp.1 = bf16[256,2048]{1,0:T(8,128)(2,1)} custom-call(bf16[256,2048]{1,0:T(8,128)(2,1)} %multiply_convert_fusion.xn_ref, f32[256,2048]{1,0:T(8,128)} %copy-done.3, bf16[2048,4096]{1,0:T(8,128)(2,1)} %wg_hbm.1, bf16[2048,4096]{1,0:T(8,128)(2,1)} %wu_hbm.1, bf16[4096,2048]{1,0:T(8,128)(2,1)} %wd_hbm.1), custom_call_target="tpu_custom_call" | custom-call | flops 51539607552 | bytes 150994944 | tf_op jit(solution)/shard_map/mlp/pallas_call | solution.py:338
  154.4 2.3 %copy.22 = bf16[256,2048]{1,0:T(8,128)(2,1)} copy(bf16[256,2048]{1,0:T(8,128)(2,1)} %mlp.1) | data formatting | bytes 2097152
  156.7 0.0 copy-done.1
  (6 shorter events, 0.0 us)
Async XLA Ops:
  0.6 12.9 %copy-start = (bf16[2048,256]{1,0:T(8,128)(2,1)S(1)}, bf16[2048,256]{1,0:T(8,128)(2,1)}, u32[]{:S(2)}) copy-start(bf16[2048,256]{1,0:T(8,128)(2,1)} %param.21) | copy-start | bytes 3145732
  1.4 3.7 %copy-start.2 = (s32[256]{0:T(256)S(1)}, s32[256]{0:T(256)}, u32[]{:S(2)}) copy-start(s32[256]{0:T(256)} %len_ref.1) | copy-start | bytes 3076
  3.0 2.8 %copy-start.4 = (bf16[256,2048]{1,0:T(8,128)(2,1)S(1)}, bf16[256,2048]{1,0:T(8,128)(2,1)}, u32[]{:S(2)}) copy-start(bf16[256,2048]{1,0:T(8,128)(2,1)} %param.13) | copy-start | bytes 3145732
  13.6 43.6 %slice-start = ((s8[8388608]{0:T(1024)(128)(4,1)}), s8[4194304]{0:T(1024)(128)(4,1)S(1)}, s32[]{:S(2)}) async-start(s8[8388608]{0:T(1024)(128)(4,1)} %bitcast.13), calls=%async_computation | async-start | bytes 8388608
  14.7 42.5 %slice-start.1 = ((s8[8388608]{0:T(1024)(128)(4,1)}), s8[4194304]{0:T(1024)(128)(4,1)S(1)}, s32[]{:S(2)}) async-start(s8[8388608]{0:T(1024)(128)(4,1)} %bitcast.13), calls=%async_computation.1 | async-start | bytes 8388608
  57.2 2.6 %copy-start.5 = (bf16[2048]{0:T(1024)(128)(2,1)S(1)}, bf16[2048]{0:T(1024)(128)(2,1)}, u32[]{:S(2)}) copy-start(bf16[2048]{0:T(1024)(128)(2,1)} %param.18) | copy-start | bytes 12292
  59.8 1.3 copy-start.3
  62.4 94.3 %copy-start.1 = (bf16[2048,256]{1,0:T(8,128)(2,1)S(1)}, bf16[2048,256]{1,0:T(8,128)(2,1)}, u32[]{:S(2)}) copy-start(bf16[2048,256]{1,0:T(8,128)(2,1)} %param.21) | copy-start | bytes 3145732

commit v3 on v0

v3 whole, which is shorter than its diff:
```python
import functools

import jax
import jax.numpy as jnp
from jax import lax
from jax.experimental import pallas as pl
from jax.experimental.pallas import tpu as pltpu
from jax.sharding import PartitionSpec as P

GROUP = 16
RING = 3
GRAIN = 16
TILE = 128
PROJ_BLOCK = 512
NORM_ROWS = 32
LANES = 128
PARTS = 2


def rms_scale(values, gain_ref, store):
    wide_vals = values.astype(jnp.float32)
    inv_rms = lax.rsqrt(jnp.mean(wide_vals * wide_vals, axis=-1, keepdims=True) + 1e-6)
    gain = 1.0 + gain_ref[...].astype(jnp.float32)
    for i in range(gain.shape[0]):
        cols = slice(i * LANES, (i + 1) * LANES)
        store(cols, (wide_vals[:, cols] * inv_rms * gain[i:i + 1, :]).astype(jnp.bfloat16))


def rope_tables(positions, head_dim):
    half_dim = head_dim // 2
    inv_freq = 10000.0 ** (-2.0 * jnp.arange(half_dim, dtype=jnp.float32) / head_dim)
    angles = positions.astype(jnp.float32)[:, None] * inv_freq[None, :]
    return jnp.cos(angles), jnp.sin(angles)


def plan_rows(cache_len):
    rows = cache_len.shape[0] // PARTS
    key = cache_len.reshape(PARTS, rows) * rows + jnp.arange(rows, dtype=jnp.int32)
    place = jnp.arange(rows + RING * GROUP, dtype=jnp.int32)
    rank = jnp.sum((key[:, None, :] < key[:, :, None]).astype(jnp.int32), axis=2)
    here = rank[:, None, :] == place[:, None]
    return jnp.sum(jnp.where(here, key[:, None, :], 0), axis=2)


def attend_kernel(part, plan_ref, x_ref, gm_ref, wo_hbm, k_hbm, v_hbm, *refs):
    if part == 0:
        (ga_ref, cos_ref, sin_ref, wq_hbm, wk_hbm, wv_hbm,
         xmid_ref, xn_ref, knew_ref, vnew_ref, qrest_ref,
         a_buf, wo_buf, o_buf, k_buf, v_buf, s_buf, kn_buf, vn_buf, wo_sem, k_sem, v_sem,
         in_buf, q_buf, wq_buf, wk_buf, wv_buf, wq_sem, wkv_sem) = refs
    else:
        (q_buf, knew_ref, vnew_ref, xmid_ref, xn_ref,
         a_buf, wo_buf, o_buf, k_buf, v_buf, s_buf, kn_buf, vn_buf, wo_sem, k_sem, v_sem) = refs
    rows, width = xmid_ref.shape
    cap, dim = k_hbm.shape[1:]
    heads = q_buf.shape[1] // rows
    row_base = part * rows
    num_groups = rows // GROUP
    num_blocks = width // PROJ_BLOCK
    per_block = PROJ_BLOCK // dim
    low, high = slice(0, dim // 2), slice(dim // 2, dim)

    def block_copy(src_hbm, dst_buf, sems, block):
        cols = pl.ds(pl.multiple_of(block * PROJ_BLOCK, PROJ_BLOCK), PROJ_BLOCK)
        return pltpu.make_async_copy(src_hbm.at[:, cols], dst_buf.at[block], sems.at[block])

    def length(place):
        return lax.div(plan_ref[part, place], rows)

    def row_of(place):
        return lax.rem(plan_ref[part, place], rows)

    def used(place):
        return pl.multiple_of((length(place) + (GRAIN - 1)) & ~(GRAIN - 1), GRAIN)

    def start(src_hbm, dst_buf, sems, group):
        ring = lax.rem(group, RING)
        for lane in range(GROUP):
            place = group * GROUP + lane
            base = pl.multiple_of((ring * GROUP + lane) * cap, cap)
            pltpu.make_async_copy(src_hbm.at[row_of(place) + row_base, pl.ds(0, used(place)), :],
                                  dst_buf.at[pl.ds(base, used(place)), :], sems.at[ring]).start()

    def wait(dst_buf, sems, group):
        ring = lax.rem(group, RING)
        total = sum(used(group * GROUP + lane) for lane in range(GROUP))
        whole = dst_buf.at[pl.ds(0, pl.multiple_of(total, GRAIN)), :]
        pltpu.make_async_copy(whole, whole, sems.at[ring]).wait()

    def head_rows(row):
        return pl.ds(pl.multiple_of(row * heads, heads), heads)

    def load_query(row):
        return jnp.concatenate([q_buf[0, head_rows(row), :], q_buf[1, head_rows(row), :]], axis=-1)

    def scores(group, span):
        ring = lax.rem(group, RING)
        for lane in range(GROUP):
            base = pl.multiple_of((ring * GROUP + lane) * cap, cap)
            query = load_query(row_of(group * GROUP + lane)).astype(jnp.bfloat16)
            s_buf[lax.rem(group, 2), lane, :, pl.ds(0, span)] = lax.dot_general(
                query, k_buf[pl.ds(base, span), :], (((1,), (1,)), ((), ())), preferred_element_type=jnp.float32)

    def outputs(group, span):
        ring = lax.rem(group, RING)
        column = lax.broadcasted_iota(jnp.int32, (heads, span), 1)
        for lane in range(GROUP):
            place = group * GROUP + lane
            row = row_of(place)
            base = pl.multiple_of((ring * GROUP + lane) * cap, cap)
            score = jnp.where(column < length(place), s_buf[lax.rem(group, 2), lane, :, pl.ds(0, span)], -jnp.inf)
            new_score = jnp.sum(load_query(row) * kn_buf[pl.ds(row, 1), :], axis=-1, keepdims=True)
            peak = jnp.maximum(jnp.max(score, axis=-1, keepdims=True), new_score)
            weight = jnp.exp(score - peak)
            new_weight = jnp.exp(new_score - peak)
            scale = 1.0 / (jnp.sum(weight, axis=-1, keepdims=True) + new_weight)
            prob = (weight * scale).astype(jnp.bfloat16)
            new_prob = (new_weight * scale).astype(jnp.bfloat16).astype(jnp.float32)
            mixed = jnp.dot(prob, v_buf[pl.ds(base, span), :], preferred_element_type=jnp.float32)
            mixed = mixed + new_prob * vn_buf[pl.ds(row, 1), :]
            o_buf[0, head_rows(row), :] = mixed[:, low]
            o_buf[1, head_rows(row), :] = mixed[:, high]

    def by_span(group, run):
        tiles = lax.div(length(group * GROUP + GROUP - 1) + (TILE - 1), TILE)
        for count in range(1, cap // TILE + 1):
            least = 0 if count == 1 else count

            @pl.when((tiles >= least) & (tiles <= count))
            def _(count=count):
                run(count * TILE)

    if part == 0:
        kv_copies = (pltpu.make_async_copy(wk_hbm, wk_buf, wkv_sem.at[0]),
                     pltpu.make_async_copy(wv_hbm, wv_buf, wkv_sem.at[1]))
        for copy in kv_copies:
            copy.start()
        for block in range(num_blocks):
            block_copy(wq_hbm, wq_buf, wq_sem, block).start()
    for group in range(RING):
        start(k_hbm, k_buf, k_sem, group)

    def clear(part, carry):
        span = pl.ds(pl.multiple_of(part * cap, cap), cap)
        v_buf[span, :] = jnp.zeros((cap, dim), v_buf.dtype)
        return carry

    lax.fori_loop(0, RING * GROUP, clear, 0)
    for group in range(RING):
        start(v_hbm, v_buf, v_sem, group)
    for block in range(num_blocks):
        block_copy(wo_hbm, wo_buf, wo_sem, block).start()

    def norm(from_ref, gain_ref, to_ref, count):
        def body(step, carry):
            span = pl.ds(pl.multiple_of(step * NORM_ROWS, NORM_ROWS), NORM_ROWS)

            def store(cols, values):
                to_ref[span, cols] = values

            rms_scale(from_ref[span, :], gain_ref, store)
            return carry

        lax.fori_loop(0, count // NORM_ROWS, body, 0)

    def turn(values):
        cos_t, sin_t = cos_ref[...], sin_ref[...]
        return (values[:, low] * cos_t - values[:, high] * sin_t,
                values[:, high] * cos_t + values[:, low] * sin_t)

    def project(block, carry):
        block_copy(wq_hbm, wq_buf, wq_sem, block).wait()
        lin = jnp.dot(in_buf[...], wq_buf[block], preferred_element_type=jnp.float32)
        for i in range(per_block):
            place = pl.ds(block * per_block + i, rows, stride=heads)
            for side, piece in enumerate(turn(lin[:, i * dim:(i + 1) * dim])):
                piece = (piece * dim ** -0.5).astype(jnp.bfloat16).astype(jnp.float32)
                q_buf[side, place, :] = piece[:rows]
                qrest_ref[side, place, :] = piece[rows:]
        return carry

    if part == 0:
        norm(x_ref, ga_ref, in_buf, PARTS * rows)
        for copy in kv_copies:
            copy.wait()
        k_lin = jnp.dot(in_buf[...], wk_buf[...], preferred_element_type=jnp.float32)
        for piece, span in zip(turn(k_lin), (low, high)):
            knew_ref[:, span] = piece.astype(jnp.bfloat16)
        vnew_ref[...] = jnp.dot(in_buf[...], wv_buf[...], preferred_element_type=jnp.float32).astype(jnp.bfloat16)
        lax.fori_loop(0, num_blocks, project, 0)
    kn_buf[...] = knew_ref[pl.ds(row_base, rows), :].astype(jnp.float32)
    vn_buf[...] = vnew_ref[pl.ds(row_base, rows), :].astype(jnp.float32)

    wait(k_buf, k_sem, 0)
    by_span(0, lambda span: scores(0, span))

    def step(group, carry):
        start(k_hbm, k_buf, k_sem, group + RING)
        wait(k_buf, k_sem, group + 1)
        wait(v_buf, v_sem, group)

        def run(span):
            scores(group + 1, span)
            outputs(group, span)

        by_span(group + 1, run)
        start(v_hbm, v_buf, v_sem, group + RING)
        return carry

    lax.fori_loop(0, num_groups - 1, step, 0)
    wait(v_buf, v_sem, num_groups - 1)
    by_span(num_groups - 1, lambda span: outputs(num_groups - 1, span))

    for head in range(heads):
        for side in range(2):
            first = head * dim + side * (dim // 2)
            a_buf[:, first:first + dim // 2] = o_buf[side, pl.ds(head, rows, stride=heads), :].astype(jnp.bfloat16)

    def mix(block, carry):
        block_copy(wo_hbm, wo_buf, wo_sem, block).wait()
        cols = pl.ds(pl.multiple_of(block * PROJ_BLOCK, PROJ_BLOCK), PROJ_BLOCK)
        mixed = jnp.dot(a_buf[...], wo_buf[block], preferred_element_type=jnp.float32)
        xmid_ref[:, cols] = x_ref[pl.ds(row_base, rows), cols].astype(jnp.float32) + mixed
        return carry

    lax.fori_loop(0, num_blocks, mix, 0)

    norm(xmid_ref, gm_ref, xn_ref, rows)


def attention_part(part, plan, hidden_in, k_cache, v_cache, norm_mlp, w_o, q_new=(), proj=()):
    cap, dim = k_cache.shape[1:]
    width = hidden_in.shape[1]
    rows = hidden_in.shape[0] // PARTS
    heads = w_o.shape[0] // dim
    num_blocks = width // PROJ_BLOCK
    smem = pl.BlockSpec(memory_space=pltpu.SMEM)
    vmem = pl.BlockSpec(memory_space=pltpu.VMEM)
    hbm = pl.BlockSpec(memory_space=pl.ANY)
    weights = [pltpu.VMEM((num_blocks, width, PROJ_BLOCK), jnp.bfloat16), pltpu.SemaphoreType.DMA((num_blocks,))]
    queries = (2, rows * heads, dim // 2)
    out_shape = [jax.ShapeDtypeStruct((rows, width), jnp.float32), jax.ShapeDtypeStruct((rows, width), jnp.bfloat16)]
    scratch_shapes = [
        pltpu.VMEM((rows, width), jnp.bfloat16),
        weights[0],
        pltpu.VMEM(queries, jnp.float32),
        pltpu.VMEM((RING * GROUP * cap, dim), jnp.bfloat16),
        pltpu.VMEM((RING * GROUP * cap, dim), jnp.bfloat16),
        pltpu.VMEM((2, GROUP, heads, cap), jnp.float32),
        pltpu.VMEM((rows, dim), jnp.float32),
        pltpu.VMEM((rows, dim), jnp.float32),
        weights[1],
        pltpu.SemaphoreType.DMA((RING,)),
        pltpu.SemaphoreType.DMA((RING,)),
    ]
    if part == 0:
        extra_specs = [vmem] * 3 + [hbm] * 3
        out_shape += [jax.ShapeDtypeStruct((PARTS * rows, dim), jnp.bfloat16)] * 2
        out_shape += [jax.ShapeDtypeStruct(queries, jnp.float32)]
        scratch_shapes += [
            pltpu.VMEM((PARTS * rows, width), jnp.bfloat16),
            pltpu.VMEM(queries, jnp.float32),
            weights[0],
            pltpu.VMEM((width, dim), jnp.bfloat16),
            pltpu.VMEM((width, dim), jnp.bfloat16),
            weights[1],
            pltpu.SemaphoreType.DMA((2,)),
        ]
    else:
        extra_specs = [vmem] * 3
    return pl.pallas_call(
        functools.partial(attend_kernel, part),
        name='attend',
        out_shape=out_shape,
        in_specs=[smem, vmem, vmem, hbm, hbm, hbm] + extra_specs,
        out_specs=[vmem] * len(out_shape),
        scratch_shapes=scratch_shapes,
        compiler_params=pltpu.CompilerParams(vmem_limit_bytes=62 * 1024 * 1024),
        cost_estimate=pl.CostEstimate(flops=4 * rows * width * width + 4 * rows * heads * dim * cap,
                                      bytes_accessed=2 * rows * cap * dim * 2 + 4 * width * width,
                                      transcendentals=rows * heads * cap),
    )(plan, hidden_in, norm_mlp.reshape(-1, LANES), w_o, k_cache, v_cache, *q_new, *proj)


HID_BLOCK = 512
OUT_BLOCK = 512
PAIR = 2
WEIGHT_RING = 2 * PAIR
MESH = pl.DeviceIdType.MESH
FAR, PARTNER, OWN = 0, 2, 3


def mlp_kernel(xn0_ref, xn1_ref, xmid0_ref, xmid1_ref, far_ref, wg_hbm, wu_hbm, wd_hbm, out_ref,
               x_all, h_buf, g_buf, u_buf, wg_buf, wu_buf, wd_buf, part, d_recv, c_recv, p_recv,
               w_sem, wd_sem, send_sem, recv_sem):
    half, width = xn0_ref.shape
    rows = 2 * half
    hidden = wg_hbm.shape[1]
    num_hid = hidden // HID_BLOCK
    num_pairs = num_hid // PAIR
    num_out = width // OUT_BLOCK
    num_steps = 4 * num_hid
    me = lax.axis_index('tp')
    partner = me + 1 - 2 * lax.rem(me, 2)
    counter = lax.rem(me + 2, 4)

    barrier = pltpu.get_barrier_semaphore()
    for peer in (partner, counter):
        pl.semaphore_signal(barrier, inc=1, device_id={'tp': peer}, device_id_type=MESH)

    def weight_copies(step):
        slot = lax.rem(step, WEIGHT_RING)
        cols = pl.ds(pl.multiple_of(lax.rem(step, num_hid) * HID_BLOCK, HID_BLOCK), HID_BLOCK)
        return (pltpu.make_async_copy(wg_hbm.at[:, cols], wg_buf.at[slot], w_sem.at[slot, 0]),
                pltpu.make_async_copy(wu_hbm.at[:, cols], wu_buf.at[slot], w_sem.at[slot, 1]))

    def down_copy(block):
        cols = pl.ds(pl.multiple_of(block * OUT_BLOCK, OUT_BLOCK), OUT_BLOCK)
        return pltpu.make_async_copy(wd_hbm.at[:, cols], wd_buf.at[block], wd_sem.at[block])

    def remote(src, dst, index, peer):
        return pltpu.make_async_remote_copy(
            src_ref=src, dst_ref=dst, send_sem=send_sem.at[index], recv_sem=recv_sem.at[index],
            device_id={'tp': peer}, device_id_type=MESH)

    top, bottom = pl.ds(0, half), pl.ds(half, half)
    gather_partner = [remote(ref, x_all.at[PARTNER, span, :], i, partner)
                      for i, (ref, span) in enumerate(((xn0_ref, top), (xn1_ref, bottom)))]
    gather_counter = remote(xn1_ref, x_all.at[FAR + 1, top, :], 2, counter)
    forward = [remote(far_ref, x_all.at[FAR, bottom, :], 3, partner),
               remote(x_all.at[FAR + 1, top, :], x_all.at[FAR + 1, bottom, :], 4, partner)]

    def cross(i, n):
        return remote(part.at[FAR + i, n, bottom, :], d_recv.at[i, n], 5 + i * num_out + n, partner)

    def home(i, n):
        return remote(part.at[FAR + i, n, top, :], c_recv.at[i, n], 5 + (2 + i) * num_out + n, counter)

    def side(n):
        return remote(part.at[PARTNER, n], p_recv.at[n], 5 + 4 * num_out + n, partner)

    for step in range(WEIGHT_RING):
        for copy in weight_copies(step):
            copy.start()
    pl.semaphore_wait(barrier, 2)
    forward[0].start()
    gather_counter.start()
    for copy in gather_partner:
        copy.start()
    x_all[FAR, top, :] = far_ref[...]
    x_all[OWN, top, :] = xn0_ref[...]
    x_all[OWN, bottom, :] = xn1_ref[...]

    def activate(keep, pair):
        for b in range(PAIR):
            first = (pair * PAIR + b) * HID_BLOCK
            cols = pl.ds(first if isinstance(first, int) else pl.multiple_of(first, HID_BLOCK), HID_BLOCK)
            h_buf[:, cols] = (jax.nn.gelu(g_buf[keep, b], approximate=True) * u_buf[keep, b]).astype(jnp.bfloat16)

    def down(number, n):
        part[number, n] = jnp.dot(h_buf[:, :hidden], wd_buf[n], preferred_element_type=jnp.float32)

    def finish(i, n):
        cross(i, n).wait_recv()
        part[FAR + i, n, top, :] = part[FAR + i, n, top, :] + d_recv[i, n]
        home(i, n).start()

    def one_pass(number, carry):
        is_partner = number == PARTNER
        is_far = number < PARTNER
        far = number - FAR

        @pl.when(is_partner)
        def _():
            for copy in gather_partner:
                copy.wait_recv()

        for i in range(2):
            @pl.when(number == FAR + i)
            def _(i=i):
                forward[i].wait_recv()

        def hidden_pair(pair, carry):
            first = number * num_hid + pair * PAIR
            keep = lax.rem(pair, 2)

            @pl.when(number == 0)
            def _():
                down_copy(pair).start()

            for b in range(PAIR):
                for copy in weight_copies(first + b):
                    copy.wait()
            for b in range(PAIR):
                slot = lax.rem(first + b, WEIGHT_RING)
                g_buf[keep, b] = jnp.dot(x_all[number], wg_buf[slot], preferred_element_type=jnp.float32)
                u_buf[keep, b] = jnp.dot(x_all[number], wu_buf[slot], preferred_element_type=jnp.float32)
                for copy in weight_copies(first + b + WEIGHT_RING):
                    copy.start()
            activate(1 - keep, lax.rem(pair + num_pairs, num_pairs + 1))

            @pl.when((pair == 0) & (number > FAR) & (number <= PARTNER))
            def _():
                for n in range(num_out // 2, num_out):
                    finish(far - 1, n)
            return carry

        lax.fori_loop(0, num_pairs, hidden_pair, 0)

        @pl.when(number == 0)
        def _():
            for n in range(num_out):
                down_copy(n).wait()

        activate((num_pairs - 1) % 2, num_pairs - 1)
        for n in range(num_out // 2):
            down(number, n)

        @pl.when(is_partner)
        def _():
            for n in range(num_out // 2):
                side(n).start()

        @pl.when(is_far)
        def _():
            for n in range(num_out // 2):
                cross(far, n).start()

        for n in range(num_out // 2, num_out):
            down(number, n)

        @pl.when(is_partner)
        def _():
            for n in range(num_out // 2, num_out):
                side(n).start()

        @pl.when(is_far)
        def _():
            for n in range(num_out // 2, num_out):
                cross(far, n).start()
            for n in range(num_out // 2):
                finish(far, n)

        @pl.when(number == FAR)
        def _():
            gather_counter.wait_recv()
            forward[1].start()
        return carry

    lax.fori_loop(0, 4, one_pass, 0)

    xmid = (xmid0_ref, xmid1_ref)

    def settle(n, carry):
        cols = pl.ds(pl.multiple_of(n * OUT_BLOCK, OUT_BLOCK), OUT_BLOCK)
        side(n).wait_recv()
        for i in range(2):
            span = pl.ds(i * half, half)
            home(i, n).wait_recv()
            total = part[OWN, n, span, :] + p_recv[n, span, :] + c_recv[i, n]
            out_ref[span, cols] = (xmid[i][:, cols] + total).astype(jnp.bfloat16)
        return carry

    lax.fori_loop(0, num_out, settle, 0)

    for step in range(num_steps, num_steps + WEIGHT_RING):
        for copy in weight_copies(step):
            copy.wait()
    gather_counter.wait_send()
    for i in range(2):
        gather_partner[i].wait_send()
        forward[i].wait_send()

    def drain(n, carry):
        side(n).wait_send()
        for i in range(2):
            cross(i, n).wait_send()
            home(i, n).wait_send()
        return carry

    lax.fori_loop(0, num_out, drain, 0)


def mlp_block(xn_mid, x_mid, far, w_gate, w_up, w_down):
    half, width = far.shape
    rows = 2 * half
    hidden = w_gate.shape[1]
    num_out = width // OUT_BLOCK
    num_copies = 5 + 5 * num_out
    vmem = pl.BlockSpec(memory_space=pltpu.VMEM)
    hbm = pl.BlockSpec(memory_space=pl.ANY)
    return pl.pallas_call(
        mlp_kernel,
        name='mlp',
        out_shape=jax.ShapeDtypeStruct((rows, width), jnp.bfloat16),
        in_specs=[vmem] * 5 + [hbm] * 3,
        out_specs=vmem,
        scratch_shapes=[
            pltpu.VMEM((4, rows, width), jnp.bfloat16),
            pltpu.VMEM((rows, hidden + PAIR * HID_BLOCK), jnp.bfloat16),
            pltpu.VMEM((2, PAIR, rows, HID_BLOCK), jnp.float32),
            pltpu.VMEM((2, PAIR, rows, HID_BLOCK), jnp.float32),
            pltpu.VMEM((WEIGHT_RING, width, HID_BLOCK), jnp.bfloat16),
            pltpu.VMEM((WEIGHT_RING, width, HID_BLOCK), jnp.bfloat16),
            pltpu.VMEM((num_out, hidden, OUT_BLOCK), jnp.bfloat16),
            pltpu.VMEM((4, num_out, rows, OUT_BLOCK), jnp.float32),
            pltpu.VMEM((2, num_out, half, OUT_BLOCK), jnp.float32),
            pltpu.VMEM((2, num_out, half, OUT_BLOCK), jnp.float32),
            pltpu.VMEM((num_out, rows, OUT_BLOCK), jnp.float32),
            pltpu.SemaphoreType.DMA((WEIGHT_RING, 2)),
            pltpu.SemaphoreType.DMA((num_out,)),
            pltpu.SemaphoreType.DMA((num_copies,)),
            pltpu.SemaphoreType.DMA((num_copies,)),
        ],
        compiler_params=pltpu.CompilerParams(collective_id=0, has_side_effects=True,
                                             vmem_limit_bytes=67043328),
        cost_estimate=pl.CostEstimate(flops=24 * rows * width * hidden,
                                      bytes_accessed=9 * width * hidden * 2,
                                      transcendentals=4 * rows * hidden),
    )(*xn_mid, *x_mid, far, w_gate, w_up, w_down)


def solution(mesh):
    row_spec = P(('dp', 'tp'), None)
    cache_spec = P(('dp', 'tp'), None, None)
    full_vec = P(None)
    full_mat = P(None, None)

    def per_device(hidden_in, k_cache, v_cache, cache_len, norm_attn, norm_mlp, w_q, w_k, w_v, w_o, w_gate, w_up, w_down):
        cos_t, sin_t = rope_tables(cache_len, w_k.shape[1])
        plan = plan_rows(cache_len)
        common = (plan, hidden_in, k_cache, v_cache, norm_mlp, w_o)
        x_first, xn_first, k_new, v_new, q_rest = attention_part(
            0, *common, proj=(norm_attn.reshape(-1, LANES), cos_t, sin_t, w_q, w_k, w_v))
        far = lax.ppermute(xn_first, 'tp', [(0, 2), (1, 3), (2, 0), (3, 1)])
        x_last, xn_last = attention_part(1, *common, q_new=(q_rest, k_new, v_new))
        hidden_out = mlp_block((xn_first, xn_last), (x_first, x_last), far, w_gate, w_up, w_down)
        return hidden_out, k_new, v_new

    return jax.shard_map(
        per_device,
        mesh=mesh,
        in_specs=(row_spec, cache_spec, cache_spec, P(('dp', 'tp')), full_vec, full_vec,
                  full_mat, full_mat, full_mat, full_mat, P(None, 'tp'), P(None, 'tp'), P('tp', None)),
        out_specs=(row_spec, row_spec, row_spec),
        check_vma=False,
    )
```

time: 274 us -> 132 us (0.48)
  matrix products: 144 us -> 0 us
  Pallas kernels: 0 us -> 123 us
  waiting for transfers between devices: 98.1 us -> 0.01 us
  between operations: 14.2 us -> 0.67 us
  other arithmetic: 11.6 us -> 3.56 us
  local copies, waits for them, and re-layouts: 5.82 us -> 2.3 us
  starting transfers between devices: 0.08 us -> 3.01 us
    dot_general x10 -> x0, matrix products: 144 us -> none  [the longest x1 28.7 us: per_device(): up_act = jnp.dot(group_rows, w_up, preferred_element_type=jnp.float32)]
    pallas_call x0 -> x3, Pallas kernels: none -> 123 us  [the longest x1 75.8 us: mlp_block(): pl.pallas_call(mlp_kernel, name='mlp', out_shape=jax.ShapeDtypeStruct((ro...]
    reduce_scatter x1 -> x0, waiting for transfers between devices: 63.6 us -> none  [per_device(): down_sum = lax.psum_scatter(part_sum, 'tp', scatter_dimension=0, tiled=True)]
    all_gather x1 -> x0, waiting for transfers between devices: 34.4 us -> none  [per_device(): group_rows = lax.all_gather(xn_mid, 'tp', axis=0, tiled=True)]
    convert_element_type x3 -> x0, other arithmetic: 4.07 us -> none  [the longest x1 2.8 us: per_device(): return ((x_mid + down_sum).astype(jnp.bfloat16), k_new, v_new)]
    ppermute x0 -> x1, starting transfers between devices: none -> 3.01 us  [per_device(): far = lax.ppermute(xn_first, 'tp', [(0, 2), (1, 3), (2, 0), (3, 1)])]
  transfers between devices with their start and end apart: 2 -> 1, of which waited for: 2 -> 0; matrix products, arithmetic and copies ran while one was open for 0% -> 0% of each run, Pallas kernels for 0% -> 16%
where the time goes in v3:
time: 132 us; the launch traced here: 133 us
  Pallas kernels  123 us (93%)
  other arithmetic  3.56 us (3%)
  starting transfers between devices  3.01 us (2%)
  local copies, waits for them, and re-layouts  2.3 us (2%)
    pallas_call x1, Pallas kernels, mlp_block(): pl.pallas_call(mlp_kernel, name='mlp', out_shape=jax.ShapeDtypeStruct((ro...  75.8 us
    pallas_call x2, Pallas kernels, attention_part(): pl.pallas_call(functools.partial(attend_kernel, part), name='attend', out...  47.5 us
    ppermute x1, starting transfers between devices, per_device(): far = lax.ppermute(xn_first, 'tp', [(0, 2), (1, 3), (2, 0), (3, 1)])  3.01 us
  transfers between devices with their start and end apart: 1, of which 0 were waited for; matrix products, arithmetic and copies ran while one was open for 0% of the time, Pallas kernels for 16%

profile of v3, /device:TPU:0, one launch (start us, length us, event | category | flops | bytes accessed | tf_op | source)
XLA Modules:
  0.0 132.8 jit_solution(7009565776487751381)
XLA Ops:
  0.6 0.7 bitcast_add_fusion
  1.3 0.7 convert_element_type.7
  2.0 0.2 convert_reduce_fusion
  2.2 0.7 select_reduce_fusion.plan_ref
  2.9 1.3 multiply_sine_fusion
  4.2 26.5 %attend.2 = (f32[128,2048]{1,0:T(8,128)}, bf16[128,2048]{1,0:T(8,128)(2,1)}, bf16[256,256]{1,0:T(8,128)(2,1)}, bf16[256,256]{1,0:T(8,128)(2,1)}, f32[2,1024,128]{2,1,0:T(8,128)}) custom-call(s32[2,176]{1,0:T(2,128)} %select_reduce_fusion.plan_ref, bf16[256,2048]{1,0:T(8,128)(2,1)} %x_ref.3, bf16[16,128]{1,0:T(8,128)(2,1)} %bitcast.4, ...), custom_call_target="tpu_custom_call" | custom-call | flops 2684354560 | bytes 83886080 | tf_op jit(solution)/shard_map/attend/pallas_call | solution.py:271
  30.7 3.0 %collective-permute-start = (bf16[128,2048]{1,0:T(8,128)(2,1)}, bf16[128,2048]{1,0:T(8,128)(2,1)}, u32[]{:S(2)}, u32[]{:S(2)}) collective-permute-start(bf16[128,2048]{1,0:T(8,128)(2,1)} %get-tuple-element.10.xn0_ref), channel_id=1, source_target_pairs={{0,2},{1,3},{2,0},{3,1},{4,6},{5,7},{6,4},{7,5}} | collective-permute-start | bytes 1572872 | tf_op jit(solution)/shard_map/ppermute | solution.py:535
  33.7 21.0 %attend.3 = (f32[128,2048]{1,0:T(8,128)}, bf16[128,2048]{1,0:T(8,128)(2,1)}) custom-call(s32[2,176]{1,0:T(2,128)} %select_reduce_fusion.plan_ref, bf16[256,2048]{1,0:T(8,128)(2,1)} %x_ref.3, bf16[16,128]{1,0:T(8,128)(2,1)} %bitcast.5, bf16[2048,2048]{1,0:T(8,128)(2,1)} %wo_hbm.3, bf16[256,512,256]{2,1,0:T(8,128)(2,1)} %k_hbm.3, ...), custom_call_target="tpu_custom_call" | custom-call | flops 2684354560 | bytes 83886080 | tf_op jit(solution)/shard_map/attend/pallas_call | solution.py:271
  54.7 0.0 collective-permute-done.far_ref
  54.7 75.8 %mlp.1 = bf16[256,2048]{1,0:T(8,128)(2,1)} custom-call(bf16[128,2048]{1,0:T(8,128)(2,1)} %get-tuple-element.10.xn0_ref, bf16[128,2048]{1,0:T(8,128)(2,1)} %get-tuple-element.14.xn1_ref, f32[128,2048]{1,0:T(8,128)} %get-tuple-element.15.xmid0_ref, f32[128,2048]{1,0:T(8,128)} %get-tuple-element.16.xmid1_ref, bf16[128,2048]{1,0:T(8,128)(2,1)} %collective-permute-done.far_ref, ...), custom_call_target="tpu_custom_call" | custom-call | flops 51539607552 | bytes 150994944 | tf_op jit(solution)/shard_map/mlp/pallas_call | solution.py:492
  130.5 2.3 %copy.17 = bf16[256,2048]{1,0:T(8,128)(2,1)} copy(bf16[256,2048]{1,0:T(8,128)(2,1)} %mlp.1) | data formatting | bytes 2097152
  (1 shorter events, 0.0 us)
Async XLA Ops:
  30.7 24.1 %collective-permute-start = (bf16[128,2048]{1,0:T(8,128)(2,1)}, bf16[128,2048]{1,0:T(8,128)(2,1)}, u32[]{:S(2)}, u32[]{:S(2)}) collective-permute-start(bf16[128,2048]{1,0:T(8,128)(2,1)} %get-tuple-element.10.xn0_ref), channel_id=1, source_target_pairs={{0,2},{1,3},{2,0},{3,1},{4,6},{5,7},{6,4},{7,5}} | collective-permute-start | bytes 1572872 | tf_op jit(solution)/shard_map/ppermute | solution.py:535

commit v4 on v3

--- a/solution.py
+++ b/solution.py
@@ -8,7 +8,7 @@
 from jax.sharding import PartitionSpec as P
 
 GROUP = 16
-RING = 3
+RING = 4
 GRAIN = 16
 TILE = 128
 PROJ_BLOCK = 512
@@ -37,7 +37,7 @@
     rows = cache_len.shape[0] // PARTS
     key = cache_len.reshape(PARTS, rows) * rows + jnp.arange(rows, dtype=jnp.int32)
     place = jnp.arange(rows + RING * GROUP, dtype=jnp.int32)
-    rank = jnp.sum((key[:, None, :] < key[:, :, None]).astype(jnp.int32), axis=2)
+    rank = jnp.sum((key[:, None, :] > key[:, :, None]).astype(jnp.int32), axis=2)
     here = rank[:, None, :] == place[:, None]
     return jnp.sum(jnp.where(here, key[:, None, :], 0), axis=2)
 
@@ -49,8 +49,9 @@
          a_buf, wo_buf, o_buf, k_buf, v_buf, s_buf, kn_buf, vn_buf, wo_sem, k_sem, v_sem,
          in_buf, q_buf, wq_buf, wk_buf, wv_buf, wq_sem, wkv_sem) = refs
     else:
-        (q_buf, knew_ref, vnew_ref, xmid_ref, xn_ref,
-         a_buf, wo_buf, o_buf, k_buf, v_buf, s_buf, kn_buf, vn_buf, wo_sem, k_sem, v_sem) = refs
+        (q_hbm, knew_hbm, vnew_hbm, xmid_ref, xn_ref,
+         a_buf, wo_buf, o_buf, k_buf, v_buf, s_buf, kn_buf, vn_buf, wo_sem, k_sem, v_sem,
+         x_buf, q_buf, knew_buf, vnew_buf, in_sem) = refs
     rows, width = xmid_ref.shape
     cap, dim = k_hbm.shape[1:]
     heads = q_buf.shape[1] // rows
@@ -64,17 +65,23 @@
         cols = pl.ds(pl.multiple_of(block * PROJ_BLOCK, PROJ_BLOCK), PROJ_BLOCK)
         return pltpu.make_async_copy(src_hbm.at[:, cols], dst_buf.at[block], sems.at[block])
 
+    assert rows & (rows - 1) == 0 and TILE & (TILE - 1) == 0 and RING & (RING - 1) == 0
+    row_bits, tile_bits = rows.bit_length() - 1, TILE.bit_length() - 1
+
     def length(place):
-        return lax.div(plan_ref[part, place], rows)
+        return plan_ref[part, place] >> row_bits
 
     def row_of(place):
-        return lax.rem(plan_ref[part, place], rows)
+        return plan_ref[part, place] & (rows - 1)
 
     def used(place):
         return pl.multiple_of((length(place) + (GRAIN - 1)) & ~(GRAIN - 1), GRAIN)
 
+    def tiles_of(group):
+        return jnp.maximum((length(group * GROUP) + (TILE - 1)) >> tile_bits, 1)
+
     def start(src_hbm, dst_buf, sems, group):
-        ring = lax.rem(group, RING)
+        ring = group & (RING - 1)
         for lane in range(GROUP):
             place = group * GROUP + lane
             base = pl.multiple_of((ring * GROUP + lane) * cap, cap)
@@ -82,7 +89,7 @@
                                   dst_buf.at[pl.ds(base, used(place)), :], sems.at[ring]).start()
 
     def wait(dst_buf, sems, group):
-        ring = lax.rem(group, RING)
+        ring = group & (RING - 1)
         total = sum(used(group * GROUP + lane) for lane in range(GROUP))
         whole = dst_buf.at[pl.ds(0, pl.multiple_of(total, GRAIN)), :]
         pltpu.make_async_copy(whole, whole, sems.at[ring]).wait()
@@ -94,21 +101,21 @@
         return jnp.concatenate([q_buf[0, head_rows(row), :], q_buf[1, head_rows(row), :]], axis=-1)
 
     def scores(group, span):
-        ring = lax.rem(group, RING)
+        ring = group & (RING - 1)
         for lane in range(GROUP):
             base = pl.multiple_of((ring * GROUP + lane) * cap, cap)
             query = load_query(row_of(group * GROUP + lane)).astype(jnp.bfloat16)
-            s_buf[lax.rem(group, 2), lane, :, pl.ds(0, span)] = lax.dot_general(
+            s_buf[group & 1, lane, :, pl.ds(0, span)] = lax.dot_general(
                 query, k_buf[pl.ds(base, span), :], (((1,), (1,)), ((), ())), preferred_element_type=jnp.float32)
 
     def outputs(group, span):
-        ring = lax.rem(group, RING)
+        ring = group & (RING - 1)
         column = lax.broadcasted_iota(jnp.int32, (heads, span), 1)
         for lane in range(GROUP):
             place = group * GROUP + lane
             row = row_of(place)
             base = pl.multiple_of((ring * GROUP + lane) * cap, cap)
-            score = jnp.where(column < length(place), s_buf[lax.rem(group, 2), lane, :, pl.ds(0, span)], -jnp.inf)
+            score = jnp.where(column < length(place), s_buf[group & 1, lane, :, pl.ds(0, span)], -jnp.inf)
             new_score = jnp.sum(load_query(row) * kn_buf[pl.ds(row, 1), :], axis=-1, keepdims=True)
             peak = jnp.maximum(jnp.max(score, axis=-1, keepdims=True), new_score)
             weight = jnp.exp(score - peak)
@@ -122,11 +129,9 @@
             o_buf[1, head_rows(row), :] = mixed[:, high]
 
     def by_span(group, run):
-        tiles = lax.div(length(group * GROUP + GROUP - 1) + (TILE - 1), TILE)
+        tiles = tiles_of(group)
         for count in range(1, cap // TILE + 1):
-            least = 0 if count == 1 else count
-
-            @pl.when((tiles >= least) & (tiles <= count))
+            @pl.when(tiles == count)
             def _(count=count):
                 run(count * TILE)
 
@@ -137,17 +142,28 @@
             copy.start()
         for block in range(num_blocks):
             block_copy(wq_hbm, wq_buf, wq_sem, block).start()
-    for group in range(RING):
+    else:
+        own = pl.ds(row_base, rows)
+        in_copies = [pltpu.make_async_copy(src, dst, in_sem.at[i]) for i, (src, dst) in enumerate((
+            (q_hbm, q_buf), (knew_hbm.at[own, :], knew_buf), (vnew_hbm.at[own, :], vnew_buf),
+            (x_ref.at[own, :], x_buf)))]
+        for copy in in_copies:
+            copy.start()
+    def clear(place, carry):
+        def body(tile, carry):
+            span = pl.ds(pl.multiple_of(place * cap + tile * TILE, TILE), TILE)
+            v_buf[span, :] = jnp.zeros((TILE, dim), v_buf.dtype)
+            return carry
+
+        return lax.fori_loop(used(place) >> tile_bits, tiles_of(place // GROUP), body, carry)
+
+    def fill(group, carry):
         start(k_hbm, k_buf, k_sem, group)
-
-    def clear(part, carry):
-        span = pl.ds(pl.multiple_of(part * cap, cap), cap)
-        v_buf[span, :] = jnp.zeros((cap, dim), v_buf.dtype)
-        return carry
-
-    lax.fori_loop(0, RING * GROUP, clear, 0)
-    for group in range(RING):
+        lax.fori_loop(group * GROUP, (group + 1) * GROUP, clear, 0)
         start(v_hbm, v_buf, v_sem, group)
+        return carry
+
+    lax.fori_loop(0, RING, fill, 0)
     for block in range(num_blocks):
         block_copy(wo_hbm, wo_buf, wo_sem, block).start()
 
@@ -188,23 +204,30 @@
             knew_ref[:, span] = piece.astype(jnp.bfloat16)
         vnew_ref[...] = jnp.dot(in_buf[...], wv_buf[...], preferred_element_type=jnp.float32).astype(jnp.bfloat16)
         lax.fori_loop(0, num_blocks, project, 0)
-    kn_buf[...] = knew_ref[pl.ds(row_base, rows), :].astype(jnp.float32)
-    vn_buf[...] = vnew_ref[pl.ds(row_base, rows), :].astype(jnp.float32)
+        kn_buf[...] = knew_ref[pl.ds(0, rows), :].astype(jnp.float32)
+        vn_buf[...] = vnew_ref[pl.ds(0, rows), :].astype(jnp.float32)
+        x_own = x_ref.at[pl.ds(0, rows), :]
+    else:
+        for copy in in_copies:
+            copy.wait()
+        kn_buf[...] = knew_buf[...].astype(jnp.float32)
+        vn_buf[...] = vnew_buf[...].astype(jnp.float32)
+        x_own = x_buf
 
     wait(k_buf, k_sem, 0)
     by_span(0, lambda span: scores(0, span))
 
     def step(group, carry):
-        start(k_hbm, k_buf, k_sem, group + RING)
         wait(k_buf, k_sem, group + 1)
         wait(v_buf, v_sem, group)
 
         def run(span):
             scores(group + 1, span)
             outputs(group, span)
-
-        by_span(group + 1, run)
-        start(v_hbm, v_buf, v_sem, group + RING)
+            start(k_hbm, k_buf, k_sem, group + RING)
+            start(v_hbm, v_buf, v_sem, group + RING)
+
+        by_span(group, run)
         return carry
 
     lax.fori_loop(0, num_groups - 1, step, 0)
@@ -220,7 +243,7 @@
         block_copy(wo_hbm, wo_buf, wo_sem, block).wait()
         cols = pl.ds(pl.multiple_of(block * PROJ_BLOCK, PROJ_BLOCK), PROJ_BLOCK)
         mixed = jnp.dot(a_buf[...], wo_buf[block], preferred_element_type=jnp.float32)
-        xmid_ref[:, cols] = x_ref[pl.ds(row_base, rows), cols].astype(jnp.float32) + mixed
+        xmid_ref[:, cols] = x_own[:, cols].astype(jnp.float32) + mixed
         return carry
 
     lax.fori_loop(0, num_blocks, mix, 0)
@@ -267,15 +290,22 @@
             pltpu.SemaphoreType.DMA((2,)),
         ]
     else:
-        extra_specs = [vmem] * 3
+        extra_specs = [hbm] * 3
+        scratch_shapes += [
+            pltpu.VMEM((rows, width), jnp.bfloat16),
+            pltpu.VMEM(queries, jnp.float32),
+            pltpu.VMEM((rows, dim), jnp.bfloat16),
+            pltpu.VMEM((rows, dim), jnp.bfloat16),
+            pltpu.SemaphoreType.DMA((4,)),
+        ]
     return pl.pallas_call(
         functools.partial(attend_kernel, part),
         name='attend',
         out_shape=out_shape,
-        in_specs=[smem, vmem, vmem, hbm, hbm, hbm] + extra_specs,
+        in_specs=[smem, hbm if part else vmem, vmem, hbm, hbm, hbm] + extra_specs,
         out_specs=[vmem] * len(out_shape),
         scratch_shapes=scratch_shapes,
-        compiler_params=pltpu.CompilerParams(vmem_limit_bytes=62 * 1024 * 1024),
+        compiler_params=pltpu.CompilerParams(vmem_limit_bytes=67043328),
         cost_estimate=pl.CostEstimate(flops=4 * rows * width * width + 4 * rows * heads * dim * cap,
                                       bytes_accessed=2 * rows * cap * dim * 2 + 4 * width * width,
                                       transcendentals=rows * heads * cap),
@@ -292,7 +322,7 @@
 
 def mlp_kernel(xn0_ref, xn1_ref, xmid0_ref, xmid1_ref, far_ref, wg_hbm, wu_hbm, wd_hbm, out_ref,
                x_all, h_buf, g_buf, u_buf, wg_buf, wu_buf, wd_buf, part, d_recv, c_recv, p_recv,
-               w_sem, wd_sem, send_sem, recv_sem):
+               xmid_buf, w_sem, wd_sem, in_sem, send_sem, recv_sem):
     half, width = xn0_ref.shape
     rows = 2 * half
     hidden = wg_hbm.shape[1]
@@ -342,14 +372,16 @@
     for step in range(WEIGHT_RING):
         for copy in weight_copies(step):
             copy.start()
+    in_copies = [pltpu.make_async_copy(ref, dst, in_sem.at[i]) for i, (ref, dst) in enumerate((
+        (far_ref, x_all.at[FAR, top, :]), (xn0_ref, x_all.at[OWN, top, :]), (xn1_ref, x_all.at[OWN, bottom, :]),
+        (xmid0_ref, xmid_buf.at[0]), (xmid1_ref, xmid_buf.at[1])))]
+    for copy in in_copies:
+        copy.start()
     pl.semaphore_wait(barrier, 2)
     forward[0].start()
     gather_counter.start()
     for copy in gather_partner:
         copy.start()
-    x_all[FAR, top, :] = far_ref[...]
-    x_all[OWN, top, :] = xn0_ref[...]
-    x_all[OWN, bottom, :] = xn1_ref[...]
 
     def activate(keep, pair):
         for b in range(PAIR):
@@ -370,10 +402,19 @@
         is_far = number < PARTNER
         far = number - FAR
 
+        @pl.when(number == 0)
+        def _():
+            in_copies[0].wait()
+
         @pl.when(is_partner)
         def _():
             for copy in gather_partner:
                 copy.wait_recv()
+
+        @pl.when(number == OWN)
+        def _():
+            for copy in in_copies[1:3]:
+                copy.wait()
 
         for i in range(2):
             @pl.when(number == FAR + i)
@@ -449,7 +490,8 @@
 
     lax.fori_loop(0, 4, one_pass, 0)
 
-    xmid = (xmid0_ref, xmid1_ref)
+    for copy in in_copies[3:]:
+        copy.wait()
 
     def settle(n, carry):
         cols = pl.ds(pl.multiple_of(n * OUT_BLOCK, OUT_BLOCK), OUT_BLOCK)
@@ -458,7 +500,7 @@
             span = pl.ds(i * half, half)
             home(i, n).wait_recv()
             total = part[OWN, n, span, :] + p_recv[n, span, :] + c_recv[i, n]
-            out_ref[span, cols] = (xmid[i][:, cols] + total).astype(jnp.bfloat16)
+            out_ref[span, cols] = (xmid_buf[i, :, cols] + total).astype(jnp.bfloat16)
         return carry
 
     lax.fori_loop(0, num_out, settle, 0)
@@ -493,7 +535,7 @@
         mlp_kernel,
         name='mlp',
         out_shape=jax.ShapeDtypeStruct((rows, width), jnp.bfloat16),
-        in_specs=[vmem] * 5 + [hbm] * 3,
+        in_specs=[hbm] * 8,
         out_specs=vmem,
         scratch_shapes=[
             pltpu.VMEM((4, rows, width), jnp.bfloat16),
@@ -507,8 +549,10 @@
             pltpu.VMEM((2, num_out, half, OUT_BLOCK), jnp.float32),
             pltpu.VMEM((2, num_out, half, OUT_BLOCK), jnp.float32),
             pltpu.VMEM((num_out, rows, OUT_BLOCK), jnp.float32),
+            pltpu.VMEM((2, half, width), jnp.float32),
             pltpu.SemaphoreType.DMA((WEIGHT_RING, 2)),
             pltpu.SemaphoreType.DMA((num_out,)),
+            pltpu.SemaphoreType.DMA((5,)),
             pltpu.SemaphoreType.DMA((num_copies,)),
             pltpu.SemaphoreType.DMA((num_copies,)),
         ],

time: 132 us -> 131 us (level)
    pallas_call x1, Pallas kernels: 75.8 us -> 72.9 us  [mlp_block(): pl.pallas_call(mlp_kernel, name='mlp', out_shape=jax.ShapeDtypeStruct((ro...]
  transfers between devices with their start and end apart: 1 -> 1, of which waited for: 0 -> 0; matrix products, arithmetic and copies ran while one was open for 0% -> 0% of each run, Pallas kernels for 16% -> 17%
where the time goes in v4:
time: 131 us
  Pallas kernels  122 us (93%)
  other arithmetic  3.56 us (3%)
  starting transfers between devices  3.05 us (2%)
  local copies, waits for them, and re-layouts  2.3 us (2%)
    pallas_call x1, Pallas kernels, mlp_block(): pl.pallas_call(mlp_kernel, name='mlp', out_shape=jax.ShapeDtypeStruct((ro...  72.9 us
    pallas_call x2, Pallas kernels, attention_part(): pl.pallas_call(functools.partial(attend_kernel, part), name='attend', out...  48.8 us
    ppermute x1, starting transfers between devices, per_device(): far = lax.ppermute(xn_first, 'tp', [(0, 2), (1, 3), (2, 0), (3, 1)])  3.05 us
  transfers between devices with their start and end apart: 1, of which 0 were waited for; matrix products, arithmetic and copies ran while one was open for 0% of the time, Pallas kernels for 17%

profile of v4, /device:TPU:0, one launch (start us, length us, event | category | flops | bytes accessed | tf_op | source)
XLA Modules:
  0.0 131.2 jit_solution(12604917670898031070)
XLA Ops:
  0.6 0.7 bitcast_add_fusion
  1.3 0.7 convert_element_type.7
  2.0 0.2 convert_reduce_fusion
  2.2 0.7 select_reduce_fusion.plan_ref
  2.9 1.3 multiply_sine_fusion
  4.2 26.3 %attend.2 = (f32[128,2048]{1,0:T(8,128)}, bf16[128,2048]{1,0:T(8,128)(2,1)}, bf16[256,256]{1,0:T(8,128)(2,1)}, bf16[256,256]{1,0:T(8,128)(2,1)}, f32[2,1024,128]{2,1,0:T(8,128)}) custom-call(s32[2,192]{1,0:T(2,128)} %select_reduce_fusion.plan_ref, bf16[256,2048]{1,0:T(8,128)(2,1)} %x_ref.3, bf16[16,128]{1,0:T(8,128)(2,1)} %bitcast.4, ...), custom_call_target="tpu_custom_call" | custom-call | flops 2684354560 | bytes 83886080 | tf_op jit(solution)/shard_map/attend/pallas_call | solution.py:301
  30.5 3.0 %collective-permute-start = (bf16[128,2048]{1,0:T(8,128)(2,1)}, bf16[128,2048]{1,0:T(8,128)(2,1)}, u32[]{:S(2)}, u32[]{:S(2)}) collective-permute-start(bf16[128,2048]{1,0:T(8,128)(2,1)} %get-tuple-element.10.xn0_ref), channel_id=1, source_target_pairs={{0,2},{1,3},{2,0},{3,1},{4,6},{5,7},{6,4},{7,5}} | collective-permute-start | bytes 1572872 | tf_op jit(solution)/shard_map/ppermute | solution.py:579
  33.6 22.4 %attend.3 = (f32[128,2048]{1,0:T(8,128)}, bf16[128,2048]{1,0:T(8,128)(2,1)}) custom-call(s32[2,192]{1,0:T(2,128)} %select_reduce_fusion.plan_ref, bf16[256,2048]{1,0:T(8,128)(2,1)} %x_ref.3, bf16[16,128]{1,0:T(8,128)(2,1)} %bitcast.5, bf16[2048,2048]{1,0:T(8,128)(2,1)} %wo_hbm.3, bf16[256,512,256]{2,1,0:T(8,128)(2,1)} %k_hbm.3, ...), custom_call_target="tpu_custom_call" | custom-call | flops 2684354560 | bytes 83886080 | tf_op jit(solution)/shard_map/attend/pallas_call | solution.py:301
  56.0 0.0 collective-permute-done.far_ref
  56.0 72.9 %mlp.1 = bf16[256,2048]{1,0:T(8,128)(2,1)} custom-call(bf16[128,2048]{1,0:T(8,128)(2,1)} %get-tuple-element.10.xn0_ref, bf16[128,2048]{1,0:T(8,128)(2,1)} %get-tuple-element.14.xn1_ref, f32[128,2048]{1,0:T(8,128)} %get-tuple-element.15.xmid0_ref, f32[128,2048]{1,0:T(8,128)} %get-tuple-element.16.xmid1_ref, bf16[128,2048]{1,0:T(8,128)(2,1)} %collective-permute-done.far_ref, ...), custom_call_target="tpu_custom_call" | custom-call | flops 51539607552 | bytes 150994944 | tf_op jit(solution)/shard_map/mlp/pallas_call | solution.py:534
  128.9 2.3 %copy.17 = bf16[256,2048]{1,0:T(8,128)(2,1)} copy(bf16[256,2048]{1,0:T(8,128)(2,1)} %mlp.1) | data formatting | bytes 2097152
  (1 shorter events, 0.0 us)
Async XLA Ops:
  30.5 25.5 %collective-permute-start = (bf16[128,2048]{1,0:T(8,128)(2,1)}, bf16[128,2048]{1,0:T(8,128)(2,1)}, u32[]{:S(2)}, u32[]{:S(2)}) collective-permute-start(bf16[128,2048]{1,0:T(8,128)(2,1)} %get-tuple-element.10.xn0_ref), channel_id=1, source_target_pairs={{0,2},{1,3},{2,0},{3,1},{4,6},{5,7},{6,4},{7,5}} | collective-permute-start | bytes 1572872 | tf_op jit(solution)/shard_map/ppermute | solution.py:579
